TPU v7x, 32 devices: a whole 2x2x4 slice. The times are simulated.
32 devices in a mesh: dp: 2 (over core), seq: 4 (over z), tensor: 4 (over y, x).
Axes of the slice: x: 2, y: 2, z: 4, core: 2. Of those that a mesh axis runs over, the one named last changes fastest.
Arguments:
- tokens: bfloat16 [256, 4, 5120], P('seq', 'dp'), parts along dimension 1, may hold values from -6 to 6
- w_query: bfloat16 [5120, 5120], P(None, 'tensor'), may hold values from -0.5 to 0.5, as said below
- w_key: bfloat16 [5120, 5120], P(None, 'tensor'), may hold values from -0.5 to 0.5, as said below
- w_value: bfloat16 [5120, 5120], P(None, 'tensor'), may hold values from -0.078125 to 0.078125
- w_out: bfloat16 [5120, 5120], P('tensor'), may hold values from -0.125 to 0.125
- gain_query: float32 [5120], P('tensor'), may hold values from 0.5 to 4
- gain_key: float32 [5120], P('tensor'), may hold values from 0.5 to 4
Outputs:
- attended: bfloat16 [256, 4, 5120], P(('seq', 'tensor'), 'dp'), parts along dimension 1
There are 2 independent parts, one for each index of `dp`. A program takes and returns all parts, laid end to end along the dimension named above; an argument that names none is the same for every part. Nothing has to cross between parts.
Inputs may be any that keep to these rules, and one draw needn't show every extreme that they name: `w_query`: entries of order 5120 ** -0.5 with unequal column scales. `w_key`: entries of order 5120 ** -0.5 with unequal column scales.
All inputs are finite; a program needn't handle non-finite values.
Results may differ from a plain program's by a relative error of at most 0.013.
The roundings to bfloat16 on the way count: a program that leaves them out, or rounds other values in their place, can miss the bound.
Values may be sent and summed in bfloat16 or wider, within the bound.
A program may use at most 256 MiB of HBM per device.

v0:
```python
import functools

import jax
import jax.numpy as jnp
from jax import lax
from jax.experimental import pallas as pl
from jax.experimental.pallas import tpu as pltpu
from jax.sharding import PartitionSpec as P

HEADS = 40
HEAD_DIM = 128
MESH = pl.DeviceIdType.MESH
COLS = 2 * HEAD_DIM
RING = 9
F32 = jnp.float32
BF16 = jnp.bfloat16


def block_kernel(
    ns, nt, tok, width,
    x_ref, gq_in, gk_in, wq, wk, wv, wo,
    out_ref,
    ring, wov, cos_ref, sin_ref, gq_ref, gk_ref, sq, sk, sums_out, sums_in, rqs, rks,
    qbuf, kbuf, vbuf, own_o, own_lse, oout, lse_out, oin, lse_in,
    mixed, part, rs_in,
    w_sem, wo_sem, sum_send, sum_recv, k_send, k_recv, v_send, v_recv,
    q_send, q_recv, o_send, o_recv, l_send, l_recv, rs_send, rs_recv,
):
    dp = lax.axis_index("dp")
    z = lax.axis_index("seq")
    me = lax.axis_index("tensor")
    nc = qbuf.shape[0]
    rows = 2 * tok
    oc = wov.shape[2]
    no = wov.shape[0]

    def w_copy(kind, c, slot):
        ref = (wk, wq, wv)[kind]
        return pltpu.make_async_copy(
            ref.at[:, pl.ds(pl.multiple_of(c * COLS, COLS), COLS)], ring.at[slot], w_sem.at[slot]
        )

    def wo_copy(c):
        return pltpu.make_async_copy(
            wo.at[:, pl.ds(pl.multiple_of(c * oc, oc), oc)], wov.at[c], wo_sem.at[c]
        )

    def start(i):
        slot = lax.rem(i, RING)

        @pl.when((i < 2 * nc) & (lax.rem(i, 2) == 0))
        def _():
            w_copy(0, i // 2, slot).start()

        @pl.when((i < 2 * nc) & (lax.rem(i, 2) == 1))
        def _():
            w_copy(1, i // 2, slot).start()

        @pl.when((i >= 2 * nc) & (i < 3 * nc))
        def _():
            w_copy(2, i - 2 * nc, slot).start()

        @pl.when((i >= 3 * nc) & (i < 3 * nc + no))
        def _():
            wo_copy(i - 3 * nc).start()

    for i in range(RING - 1):
        w_copy(i % 2, i // 2, i).start()

    barrier = pltpu.get_barrier_semaphore()
    peers = []
    for dz in range(ns):
        for dk in range(nt):
            if dz or dk:
                peers.append((dp, lax.rem(z + dz, ns), lax.rem(me + dk, nt)))
    for peer in peers:
        pl.semaphore_signal(barrier, inc=1, device_id=peer, device_id_type=MESH)

    def remote(src, dst, ssem, rsem, to):
        return pltpu.make_async_remote_copy(
            src_ref=src, dst_ref=dst, send_sem=ssem, recv_sem=rsem, device_id=to, device_id_type=MESH
        )

    def k_copy(c, to):
        return remote(kbuf.at[c, :, pl.ds(0, tok)], kbuf.at[c, :, pl.ds(tok, tok)], k_send.at[c], k_recv.at[c], (dp, to, me))

    def v_copy(c, to):
        return remote(vbuf.at[c, :, pl.ds(0, tok)], vbuf.at[c, :, pl.ds(tok, tok)], v_send.at[c], v_recv.at[c], (dp, to, me))

    def q_copy(c, s, to):
        return remote(qbuf.at[c, :, pl.ds(0, tok)], qbuf.at[c, :, pl.ds(s * tok, tok)], q_send.at[s - 1, c], q_recv.at[s - 1, c], (dp, to, me))

    def o_copy(c, s, to):
        return remote(oout.at[s - 1, c], oin.at[s - 1, c], o_send.at[s - 1, c], o_recv.at[s - 1, c], (dp, to, me))

    def l_copy(s, to):
        return remote(lse_out.at[s - 1], lse_in.at[s - 1], l_send.at[s - 1], l_recv.at[s - 1], (dp, to, me))

    def product(kind, i):
        slot = lax.rem(i, RING)
        start(i + RING - 1)
        w_copy(kind, 0, slot).wait()
        return jnp.dot(x_ref[...], ring[slot], preferred_element_type=F32)

    def turned(acc, gain, c, buf):
        cosine, sine = cos_ref[...], sin_ref[...]
        for h in range(2):
            y = acc[:, h * HEAD_DIM : (h + 1) * HEAD_DIM] * gain[c, :, h * HEAD_DIM : (h + 1) * HEAD_DIM]
            y = (y * cosine + pltpu.roll(y, HEAD_DIM // 2, 1) * sine).astype(BF16)
            for j in range(2):
                buf[c, j, 0:tok, h * HEAD_DIM : (h + 1) * HEAD_DIM] = y[j * tok : (j + 1) * tok]

    lanes = lax.broadcasted_iota(jnp.int32, (tok, HEAD_DIM), 1)
    half = HEAD_DIM // 2
    freqs = jnp.exp(-jnp.log(500000.0) * lax.rem(lanes, half).astype(F32) * 2.0 / HEAD_DIM)
    spot = z * tok + lax.broadcasted_iota(jnp.int32, (tok, HEAD_DIM), 0)
    angle = spot.astype(F32) * freqs
    cosine = jnp.cos(angle)
    sine = jnp.sin(angle)
    sine = jnp.where(lanes < half, -sine, sine)
    for j in range(2):
        cos_ref[j * tok : (j + 1) * tok] = cosine
        sin_ref[j * tok : (j + 1) * tok] = sine
    for c in range(nc):
        gq_ref[c] = gq_in[c * COLS : (c + 1) * COLS].reshape(1, COLS)
        gk_ref[c] = gk_in[c * COLS : (c + 1) * COLS].reshape(1, COLS)
    sq[...] = jnp.zeros_like(sq)
    sk[...] = jnp.zeros_like(sk)

    @pl.loop(0, nc)
    def _(c):
        acc = product(0, 2 * c)

        @pl.when(c == 0)
        def _():
            pl.semaphore_wait(barrier, len(peers))

        sk[...] += acc[:, :HEAD_DIM] * acc[:, :HEAD_DIM] + acc[:, HEAD_DIM:] * acc[:, HEAD_DIM:]
        turned(acc, gk_ref, c, kbuf)

        @pl.when(z == 0)
        def _():
            k_copy(c, 1).start()

        acc = product(1, 2 * c + 1)
        sq[...] += acc[:, :HEAD_DIM] * acc[:, :HEAD_DIM] + acc[:, HEAD_DIM:] * acc[:, HEAD_DIM:]
        turned(acc, gq_ref, c, qbuf)

        @pl.when(z == 3)
        def _():
            q_copy(c, 2, 1).start()
            q_copy(c, 1, 2).start()

        @pl.when(z == 2)
        def _():
            q_copy(c, 1, 1).start()

    sums_out[...] = jnp.zeros_like(sums_out)
    sums_out[0:1, :] = jnp.sum(jnp.transpose(sq[...]), axis=0, keepdims=True)
    sums_out[1:2, :] = jnp.sum(jnp.transpose(sk[...]), axis=0, keepdims=True)
    mine = z * nt + me
    sends = []
    for n, peer in enumerate(peers):
        copy = remote(sums_out, sums_in.at[n], sum_send.at[n], sum_recv.at[n], peer)
        copy.start()
        sends.append(copy)

    def scales():
        for copy in sends:
            copy.wait()

        def total(back):
            tot = sums_out[...] if back == 0 else None
            n = 0
            for dz in range(ns):
                for dk in range(nt):
                    if dz or dk:
                        if dz == back:
                            tot = sums_in[n] if tot is None else tot + sums_in[n]
                        n += 1
            return lax.rsqrt(tot / width + 1e-06)

        r0 = total(0)
        ahead = [r0, total(ns - 1), total(ns - 2)]
        factor = HEAD_DIM ** (-0.5)
        for s in range(3):
            rqs[s] = jnp.transpose(jnp.broadcast_to(ahead[s][0:1, :] * factor, (rows, rows)))
        r1 = total(1)
        low = lax.broadcasted_iota(jnp.int32, r0.shape, 1) < tok
        rks[0] = jnp.where(low, r0, pltpu.roll(r1, tok, 1))
        rks[1] = jnp.where(low, pltpu.roll(r0, tok, 1), r1)

    lane = lax.broadcasted_iota(jnp.int32, (tok, HEAD_DIM), 1)

    def attend(c, nq, nk, has_in):
        row = lax.broadcasted_iota(jnp.int32, (tok, nk * tok), 0)
        col = lax.broadcasted_iota(jnp.int32, (tok, nk * tok), 1)
        allowed = (col <= row) | (col >= tok)
        for s in range(1, nq):
            q_copy(c, s, z).wait_recv()
        if nk > 1:
            k_copy(c, z).wait_recv()
            v_copy(c, z).wait_recv()
        for j in range(2):
            for h in range(2):
                hs = slice(h * HEAD_DIM, (h + 1) * HEAD_DIM)
                u = c * 4 + j * 2 + h
                k = kbuf[c, j, 0 : nk * tok, hs]
                v = vbuf[c, j, 0 : nk * tok, hs]
                q = qbuf[c, j, 0 : nq * tok, hs]
                score = lax.dot_general(q, k, (((1,), (1,)), ((), ())), preferred_element_type=F32)
                weights, tots, tops = [], [], []
                for s in range(nq):
                    sc = score[s * tok : (s + 1) * tok]
                    sc = sc * rqs[s, j * tok : (j + 1) * tok, 0 : nk * tok] * rks[j, 1:2, 0 : nk * tok]
                    if s == 0:
                        sc = jnp.where(allowed, sc, -1e30)
                    top = jnp.max(sc, axis=1, keepdims=True)
                    e = jnp.exp(sc - top)
                    tots.append(jnp.sum(e, axis=1, keepdims=True))
                    tops.append(top)
                    weights.append(e.astype(BF16))
                w = weights[0] if nq == 1 else jnp.concatenate(weights, axis=0)
                acc = jnp.dot(w, v, preferred_element_type=F32)
                for s in range(nq):
                    o = acc[s * tok : (s + 1) * tok] / tots[s]
                    if s == 0 and not has_in:
                        mixed[j * tok : (j + 1) * tok, pl.ds(pl.multiple_of(c * COLS + h * HEAD_DIM, HEAD_DIM), HEAD_DIM)] = o.astype(BF16)
                    elif s == 0:
                        own_o[c, j, :, hs] = o
                        own_lse[...] = jnp.where(lane == u, tops[s] + jnp.log(tots[s]), own_lse[...])
                    else:
                        oout[s - 1, c, j, :, hs] = o.astype(BF16)
                        lse_out[s - 1] = jnp.where(lane == u, tops[s] + jnp.log(tots[s]), lse_out[s - 1])
        for s in range(1, nq):
            o_copy(c, s, z + s).start()

    def merge(ni):
        for s in range(1, ni + 1):
            l_copy(s, z).wait_recv()
        lses = [own_lse[...]] + [lse_in[s] for s in range(ni)]
        top = functools.reduce(jnp.maximum, lses)
        parts = [jnp.exp(v - top) for v in lses]
        tot = functools.reduce(jnp.add, parts)
        for s in range(ni + 1):
            rqs[s, 0:tok] = parts[s] / tot

        @pl.loop(0, nc)
        def _(c):
            for s in range(1, ni + 1):
                o_copy(c, s, z).wait_recv()
            for j in range(2):
                for h in range(2):
                    hs = slice(h * HEAD_DIM, (h + 1) * HEAD_DIM)
                    u = c * 4 + j * 2 + h
                    o = 0.0
                    for s in range(ni + 1):
                        share = jnp.sum(jnp.where(lane == u, rqs[s, 0:tok], 0.0), axis=1, keepdims=True)
                        o += share * (own_o[c, j, :, hs] if s == 0 else oin[s - 1, c, j, :, hs].astype(F32))
                    mixed[j * tok : (j + 1) * tok, pl.ds(pl.multiple_of(c * COLS + h * HEAD_DIM, HEAD_DIM), HEAD_DIM)] = o.astype(BF16)

    own_lse[...] = jnp.zeros_like(own_lse)
    lse_out[...] = jnp.zeros_like(lse_out)

    @pl.loop(0, nc)
    def _(c):
        acc = product(2, 2 * nc + c).astype(BF16)
        for j in range(2):
            vbuf[c, j, 0:tok, :] = acc[j * tok : (j + 1) * tok]

        @pl.when(z == 0)
        def _():
            v_copy(c, 1).start()

        @pl.when(c == 0)
        def _():
            scales()

        @pl.when(z == 0)
        def _():
            attend(c, 1, 1, False)

        @pl.when(z == 1)
        def _():
            attend(c, 3, 2, False)

        @pl.when(z == 2)
        def _():
            attend(c, 2, 1, True)

        @pl.when(z == 3)
        def _():
            attend(c, 1, 1, True)

    @pl.when(z == 1)
    def _():
        l_copy(1, 2).start()
        l_copy(2, 3).start()

    @pl.when(z == 2)
    def _():
        l_copy(1, 3).start()
        merge(1)

    @pl.when(z == 3)
    def _():
        merge(2)

    share = tok // nt

    def rs_copy(c, d):
        to = lax.rem(me + d, nt)
        return remote(
            part.at[c, :, pl.ds(pl.multiple_of(to * share, share), share)], rs_in.at[d - 1, c],
            rs_send.at[d - 1, c], rs_recv.at[d - 1, c], (dp, z, to),
        )

    @pl.loop(0, no)
    def _(c):
        wo_copy(c).wait()
        acc = jnp.dot(mixed[...], wov[c], preferred_element_type=F32).astype(BF16)
        for j in range(2):
            part[c, j] = acc[j * tok : (j + 1) * tok]
        for d in range(1, nt):
            rs_copy(c, d).start()

    @pl.loop(0, no)
    def _(c):
        for d in range(1, nt):
            rs_copy(c, d).wait_recv()
        for j in range(2):
            o = part[c, j, pl.ds(pl.multiple_of(me * share, share), share)].astype(F32)
            for d in range(1, nt):
                o += rs_in[d - 1, c, j].astype(F32)
            out_ref[j, :, pl.ds(pl.multiple_of(c * oc, oc), oc)] = o.astype(BF16)
        for d in range(1, nt):
            rs_copy(c, d).wait_send()

    @pl.loop(0, nc)
    def _(c):
        @pl.when(z == 0)
        def _():
            k_copy(c, 1).wait_send()
            v_copy(c, 1).wait_send()

        @pl.when(z == 3)
        def _():
            q_copy(c, 2, 1).wait_send()
            q_copy(c, 1, 2).wait_send()

        @pl.when(z == 2)
        def _():
            q_copy(c, 1, 1).wait_send()
            o_copy(c, 1, 3).wait_send()

        @pl.when(z == 1)
        def _():
            o_copy(c, 1, 2).wait_send()
            o_copy(c, 2, 3).wait_send()

    @pl.when(z == 2)
    def _():
        l_copy(1, 3).wait_send()

    @pl.when(z == 1)
    def _():
        l_copy(1, 2).wait_send()
        l_copy(2, 3).wait_send()


def fused(ns, nt, tokens, w_query, w_key, w_value, w_out, gain_query, gain_key):
    tok, seqs, depth = tokens.shape
    local = w_query.shape[1]
    nc = local // COLS
    oc = 1024
    no = depth // oc
    rows = tok * seqs
    width = HEADS * HEAD_DIM
    x = jnp.transpose(tokens, (1, 0, 2)).reshape(rows, depth)
    peers = ns * nt - 1
    vm = pltpu.VMEM
    dma = pltpu.SemaphoreType.DMA
    tile = (tok, HEAD_DIM)
    scratch = [
        vm((RING, depth, COLS), BF16), vm((no, local, oc), BF16),
        vm((rows, HEAD_DIM), F32), vm((rows, HEAD_DIM), F32), vm((nc, 1, COLS), F32), vm((nc, 1, COLS), F32),
        vm((rows, HEAD_DIM), F32), vm((rows, HEAD_DIM), F32),
        vm((8, rows), F32), vm((peers, 8, rows), F32),
        vm((3, rows, rows), F32), vm((2, 8, rows), F32),
        vm((nc, seqs, 3 * tok, COLS), BF16), vm((nc, seqs, 2 * tok, COLS), BF16), vm((nc, seqs, 2 * tok, COLS), BF16),
        vm((nc, seqs, tok, COLS), F32), vm(tile, F32),
        vm((2, nc, seqs, tok, COLS), BF16), vm((2,) + tile, F32),
        vm((2, nc, seqs, tok, COLS), BF16), vm((2,) + tile, F32),
        vm((rows, local), BF16), vm((no, seqs, tok, oc), BF16), vm((nt - 1, no, seqs, tok // nt, oc), BF16),
        dma((RING,)), dma((no,)), dma((peers,)), dma((peers,)),
        dma((nc,)), dma((nc,)), dma((nc,)), dma((nc,)),
        dma((2, nc)), dma((2, nc)), dma((2, nc)), dma((2, nc)), dma((2,)), dma((2,)),
        dma((nt - 1, no)), dma((nt - 1, no)),
    ]
    in_vmem = pl.BlockSpec(memory_space=pltpu.VMEM)
    anywhere = pl.BlockSpec(memory_space=pl.ANY)
    out = pl.pallas_call(
        functools.partial(block_kernel, ns, nt, tok, width),
        out_shape=jax.ShapeDtypeStruct((seqs, tok // nt, depth), BF16),
        in_specs=[in_vmem] * 3 + [anywhere] * 4,
        out_specs=in_vmem,
        scratch_shapes=scratch,
        compiler_params=pltpu.CompilerParams(collective_id=0, has_side_effects=True, vmem_limit_bytes=60 * 1024 * 1024),
    )(x, gain_query, gain_key, w_query, w_key, w_value, w_out)
    return jnp.transpose(out, (1, 0, 2))


def rotary(field, positions):
    half = HEAD_DIM // 2
    shaped = field.reshape(field.shape[0], -1, HEAD_DIM)
    freqs = jnp.exp(-jnp.log(500000.0) * jnp.arange(half, dtype=jnp.float32) * 2.0 / HEAD_DIM)
    angle = positions.astype(jnp.float32)[:, None] * freqs[None, :]
    cosine = jnp.cos(angle)[:, None, :]
    sine = jnp.sin(angle)[:, None, :]
    first = shaped[..., :half]
    second = shaped[..., half:]
    turned = jnp.concatenate(
        [first * cosine - second * sine, second * cosine + first * sine], axis=-1
    )
    return turned.reshape(field.shape[0], -1)


def local(tokens, w_query, w_key, w_value, w_out, gain_query, gain_key):
    tok_rows = tokens.shape[0]
    seq_count = tokens.shape[1]
    local_width = w_query.shape[1]
    local_heads = local_width // HEAD_DIM
    width = HEADS * HEAD_DIM
    flat = tokens.reshape(tok_rows * seq_count, tokens.shape[2])
    query = jnp.dot(flat, w_query, preferred_element_type=jnp.float32)
    key_raw = jnp.dot(flat, w_key, preferred_element_type=jnp.float32)
    sum_query, sum_key = lax.psum(
        (jnp.sum(query * query, axis=1), jnp.sum(key_raw * key_raw, axis=1)), "tensor"
    )
    value = jnp.dot(flat, w_value, preferred_element_type=jnp.float32).astype(jnp.bfloat16)
    scale_q = lax.rsqrt(sum_query / width + 1e-06)
    scale_k = lax.rsqrt(sum_key / width + 1e-06)
    my_block = lax.axis_index("seq")
    positions = my_block * tok_rows + jnp.arange(tok_rows, dtype=jnp.int32)
    row_positions = (positions[:, None] + jnp.zeros((1, seq_count), jnp.int32)).reshape(-1)
    q_normed = rotary(query * scale_q[:, None] * gain_query[None, :], row_positions).astype(
        jnp.bfloat16
    )
    k_normed = rotary(key_raw * scale_k[:, None] * gain_key[None, :], row_positions).astype(
        jnp.bfloat16
    )
    q_heads = q_normed.reshape(tok_rows, seq_count, local_heads, HEAD_DIM)
    k_local = k_normed.reshape(tok_rows, seq_count, local_width)
    v_local = value.reshape(tok_rows, seq_count, local_width)
    factor = HEAD_DIM ** (-0.5)
    piece = (
        lax.all_gather(k_local, "seq", axis=0, tiled=True),
        lax.all_gather(v_local, "seq", axis=0, tiled=True),
    )
    key_pos = jnp.arange(piece[0].shape[0], dtype=jnp.int32)
    key_block = piece[0]
    count = key_block.shape[0]
    key_heads = key_block.reshape(count, seq_count, local_heads, HEAD_DIM)
    value_heads = piece[1].reshape(count, seq_count, local_heads, HEAD_DIM)
    scores = (
        jnp.einsum("qshd,kshd->shqk", q_heads, key_heads, preferred_element_type=jnp.float32)
        * factor
    )
    allowed = (key_pos[None, None, None, :] <= positions[None, None, :, None]) & (
        key_pos[None, None, None, :] >= 0
    )
    old_max = jnp.full((seq_count, local_heads, tok_rows), -1e30, jnp.float32)
    new_max = jnp.maximum(old_max, jnp.max(jnp.where(allowed, scores, -1e30), axis=3))
    expo = jnp.where(allowed, jnp.exp(scores - new_max[..., None]), 0.0)
    new_total = jnp.sum(expo, axis=3)
    added = jnp.einsum(
        "shqk,kshd->shqd",
        expo.astype(jnp.bfloat16),
        value_heads,
        preferred_element_type=jnp.float32,
    )
    final_state = (new_max, new_total, added)
    final_max, final_total, final_acc = final_state
    mixed = (final_acc / final_total[..., None]).astype(jnp.bfloat16)
    mixed = jnp.transpose(mixed, (2, 0, 1, 3)).reshape(tok_rows, seq_count, local_width)
    return lax.psum_scatter(
        jnp.dot(mixed, w_out, preferred_element_type=jnp.float32).astype(jnp.bfloat16),
        "tensor",
        scatter_dimension=0,
        tiled=True,
    )


def solution(mesh):
    ns, nt = mesh.shape["seq"], mesh.shape["tensor"]
    step = functools.partial(fused, ns, nt) if ns == 4 and nt == 4 else local
    return jax.shard_map(
        step,
        mesh=mesh,
        in_specs=(
            P("seq", "dp", None),
            P(None, "tensor"),
            P(None, "tensor"),
            P(None, "tensor"),
            P("tensor", None),
            P("tensor"),
            P("tensor"),
        ),
        out_specs=P(("seq", "tensor"), "dp", None),
        check_vma=False,
    )
```

profile of v0, /device:TPU:24, one launch (start us, length us, event | category | flops | bytes accessed | tf_op | source)
XLA Modules:
  0.0 65.0 jit_solution(16981601227137305683)
XLA Ops:
  0.0 2.6 %copy.8 = bf16[2,64,5120]{2,1,0:T(8,128)(2,1)} copy(bf16[2,64,5120]{2,0,1:T(2,128)(2,1)} %bitcast.5) | data formatting | bytes 2621440 | tf_op jit(solution)/shard_map/transpose | solution.py:379
  2.6 60.4 %shard_map.73 = bf16[2,16,5120]{2,1,0:T(8,128)(2,1)} custom-call(bf16[128,5120]{1,0:T(8,128)(2,1)} %bitcast.3, f32[1280]{0:T(1024)} %gq_in.1, f32[1280]{0:T(1024)} %gk_in.1, bf16[5120,1280]{1,0:T(8,128)(2,1)} %wq.1, bf16[5120,1280]{1,0:T(8,128)(2,1)} %wk.1, bf16[5120,1280]{1,0:T(8,128)(2,1)} %wv.1, bf16[1280,5120]{1,0:T(8,128)(2,1)} %wo.1), custom_call_target="tpu_custom_call" | custom-call | tf_op jit(solution)/shard_map/pallas_call | solution.py:402
  63.0 2.0 %copy.9 = bf16[16,2,5120]{2,1,0:T(2,128)(2,1)} copy(bf16[16,2,5120]{2,0,1:T(8,128)(2,1)} %bitcast.4) | data formatting | bytes 655360 | tf_op jit(solution)/shard_map/transpose | solution.py:410
where the time goes:
time: 65.2 us; the launch traced here: 65 us
  Pallas kernels  60.4 us (93%)
  local copies, waits for them, and re-layouts  4.67 us (7%)
    pallas_call x1, Pallas kernels, fused(): pl.pallas_call(functools.partial(block_kernel, ns, nt, tok, width), out_s...  60.4 us
    transpose x1, local copies, waits for them, and re-layouts, fused(): x = jnp.transpose(tokens, (1, 0, 2)).reshape(rows, depth)  2.63 us
    transpose x1, local copies, waits for them, and re-layouts, fused(): return jnp.transpose(out, (1, 0, 2))  2.03 us

commit v1 on v0

v1 whole, which is shorter than its diff:
```python
import contextlib
import functools

import jax
import jax.numpy as jnp
from jax import lax
from jax.experimental import pallas as pl
from jax.experimental.pallas import tpu as pltpu
from jax.sharding import PartitionSpec as P

HEADS = 40
HEAD_DIM = 128
MESH = pl.DeviceIdType.MESH
COLS = 2 * HEAD_DIM
RING = 9
F32 = jnp.float32
BF16 = jnp.bfloat16


def scope(name):
    return contextlib.nullcontext()


def block_kernel(
    ns, nt, tok, width,
    x_hbm, gq_in, gk_in, wq, wk, wv, wo,
    out_ref,
    ring, wov, xin, xi, xs, cos_ref, sin_ref, gains, ssq,
    sums_out, sums_in, sums_far, rqs, rks,
    qk, vbuf, own_o, own_lse, oout, lse_out, lse_msg, oin, lse_in, shares,
    mixed, part, rs_in,
    x_sem, w_sem, wo_sem, sum_send, sum_recv, far_send, far_recv, k_send, k_recv, v_send, v_recv,
    q_send, q_recv, o_send, o_recv, l_send, l_recv, rs_send, rs_recv,
):
    dp = lax.axis_index("dp")
    z = lax.axis_index("seq")
    me = lax.axis_index("tensor")
    low = z < 2
    high = z >= 2
    nc = vbuf.shape[0]
    rows = 2 * tok
    oc = wov.shape[2]
    no = wov.shape[0]

    def w_copy(ref, c, slot):
        return pltpu.make_async_copy(
            ref.at[:, pl.ds(pl.multiple_of(c * COLS, COLS), COLS)], ring.at[slot], w_sem.at[slot]
        )

    def wo_copy(c):
        return pltpu.make_async_copy(
            wo.at[:, pl.ds(pl.multiple_of(c * oc, oc), oc)], wov.at[c], wo_sem.at[c]
        )

    def start(i):
        slot = lax.rem(i, RING)
        group = i // nc
        c = i - group * nc
        inside = i < 3 * nc

        @pl.when(inside & ((low & (group == 0)) | (high & (group == 1))))
        def _():
            w_copy(wk, c, slot).start()

        @pl.when(inside & (((z == 0) & (group == 1)) | ((z > 0) & (group == 2))))
        def _():
            w_copy(wv, c, slot).start()

        @pl.when(inside & (((z == 0) & (group == 2)) | ((z == 1) & (group == 1)) | (high & (group == 0))))
        def _():
            w_copy(wq, c, slot).start()

        @pl.when((i >= 3 * nc) & (i < 3 * nc + no))
        def _():
            wo_copy(i - 3 * nc).start()

    x_copy = pltpu.make_async_copy(x_hbm, xin, x_sem)
    x_copy.start()

    @pl.loop(0, RING - 1)
    def _(i):
        start(i)

    barrier = pltpu.get_barrier_semaphore()
    linked = {0: (1,), 1: (0, 2, 3), 2: (1, 3), 3: (1, 2)}
    for d in range(1, nt):
        pl.semaphore_signal(barrier, inc=1, device_id=(dp, z, lax.rem(me + d, nt)), device_id_type=MESH)
    for a in range(ns):
        hit = functools.reduce(jnp.logical_or, [z == b for b in linked[a]])

        @pl.when(hit)
        def _():
            for d in range(nt):
                pl.semaphore_signal(barrier, inc=1, device_id=(dp, a, lax.rem(me + d, nt)), device_id_type=MESH)

    def greet():
        pl.semaphore_wait(barrier, nt - 1 + nt * jnp.where(z == 0, 1, jnp.where(z == 1, 3, 2)))

    def remote(src, dst, ssem, rsem, to):
        return pltpu.make_async_remote_copy(
            src_ref=src, dst_ref=dst, send_sem=ssem, recv_sem=rsem, device_id=to, device_id_type=MESH
        )

    def k_copy(c, j, to):
        return remote(qk.at[0, c, j, pl.ds(0, tok)], qk.at[0, c, j, pl.ds(tok, tok)], k_send.at[j, c], k_recv.at[j, c], (dp, to, me))

    def v_copy(c, j, to):
        return remote(vbuf.at[c, j, pl.ds(0, tok)], vbuf.at[c, j, pl.ds(tok, tok)], v_send.at[j, c], v_recv.at[j, c], (dp, to, me))

    def q_copy(c, j, s, to):
        return remote(qk.at[1, c, j, pl.ds(0, tok)], qk.at[1, c, j, pl.ds(s * tok, tok)], q_send.at[s - 1, j, c], q_recv.at[s - 1, j, c], (dp, to, me))

    def o_copy(c, j, s, to):
        return remote(oout.at[s - 1, c, j], oin.at[s - 1, c, j], o_send.at[s - 1, j, c], o_recv.at[s - 1, j, c], (dp, to, me))

    def l_copy(j, s, to):
        return remote(lse_msg.at[j], lse_in.at[s - 1, j], l_send.at[s - 1, j], l_recv.at[s - 1, j], (dp, to, me))

    def near(g, d):
        return remote(sums_out.at[g], sums_in.at[g, d - 1], sum_send.at[g, d - 1], sum_recv.at[g, d - 1], (dp, z, lax.rem(me + d, nt)))

    def far(d, slot, ss, to):
        return remote(sums_out.at[0], sums_far.at[slot, d], far_send.at[ss, d], far_recv.at[slot, d], (dp, to, lax.rem(me + d, nt)))

    def product(i):
        slot = lax.rem(i, RING)
        start(i + RING - 1)
        with scope("wwait"):
            w_copy(wk, 0, slot).wait()
        return jnp.dot(xs[...], ring[slot], preferred_element_type=F32)

    def turned(acc, kind, c):
        cosine, sine = cos_ref[...], sin_ref[...]
        for h in range(2):
            y = acc[:, h * HEAD_DIM : (h + 1) * HEAD_DIM] * gains[kind, c, :, h * HEAD_DIM : (h + 1) * HEAD_DIM]
            y = (y * cosine + pltpu.roll(y, HEAD_DIM // 2, 1) * sine).astype(BF16)
            for j in range(2):
                qk[kind, c, j, 0:tok, h * HEAD_DIM : (h + 1) * HEAD_DIM] = y[j * tok : (j + 1) * tok]

    def finish(acc, kind, c):
        ssq[kind] += acc[:, :HEAD_DIM] * acc[:, :HEAD_DIM] + acc[:, HEAD_DIM:] * acc[:, HEAD_DIM:]
        turned(acc, kind, c)

    def keep_value(acc, c):
        v = acc.astype(BF16)
        for j in range(2):
            vbuf[c, j, 0:tok, :] = v[j * tok : (j + 1) * tok]

    with scope("init"):
        lanes = lax.broadcasted_iota(jnp.int32, (tok, HEAD_DIM), 1)
        half = HEAD_DIM // 2
        freqs = jnp.exp(-jnp.log(500000.0) * lax.rem(lanes, half).astype(F32) * 2.0 / HEAD_DIM)
        spot = z * tok + lax.broadcasted_iota(jnp.int32, (tok, HEAD_DIM), 0)
        angle = spot.astype(F32) * freqs
        cosine = jnp.cos(angle)
        sine = jnp.sin(angle)
        sine = jnp.where(lanes < half, -sine, sine)
        for j in range(2):
            cos_ref[j * tok : (j + 1) * tok] = cosine
            sin_ref[j * tok : (j + 1) * tok] = sine
        for c in range(nc):
            gains[0, c] = gk_in[c * COLS : (c + 1) * COLS].reshape(1, COLS)
            gains[1, c] = gq_in[c * COLS : (c + 1) * COLS].reshape(1, COLS)
        ssq[...] = jnp.zeros_like(ssq)
        sums_out[...] = jnp.zeros_like(sums_out)
        own_lse[...] = jnp.zeros_like(own_lse)
        lse_out[...] = jnp.zeros_like(lse_out)

    with scope("xwait"):
        x_copy.wait()
    with scope("xlay"):
        @pl.loop(0, tok // 8)
        def _(i):
            v = xin[pl.ds(pl.multiple_of(i * 8, 8), 8)]
            xi[pl.ds(pl.multiple_of(i * 16, 16), 16), :] = v.reshape(16, v.shape[-1])

        r = lax.broadcasted_iota(jnp.int32, (rows, rows), 0)
        q = lax.broadcasted_iota(jnp.int32, (rows, rows), 1)
        pick = (q == jnp.where(r < tok, 2 * r, 2 * (r - tok) + 1)).astype(F32).astype(BF16)

        half_depth = xs.shape[1] // 2
        for i in range(2):
            at = slice(i * half_depth, (i + 1) * half_depth)
            xs[:, at] = jnp.dot(pick, xi[:, at], preferred_element_type=F32).astype(BF16)

    def send_sums(g, kind):
        sums_out[g, 0:1, :] = jnp.sum(jnp.transpose(ssq[kind]), axis=0, keepdims=True)
        for d in range(1, nt):
            near(g, d).start()

    first = jnp.where(low, 0, 1)
    second = jnp.where(z == 1, 1, 0)

    with scope("g0"):
        @pl.loop(0, nc)
        def _(c):
            acc = product(c)

            @pl.when((c == 0) & (z != 1))
            def _():
                greet()

            finish(acc, first, c)

            @pl.when(z == 0)
            def _():
                k_copy(c, 0, 1).start()

            @pl.when(z == 3)
            def _():
                q_copy(c, 0, 2, 1).start()

    @pl.when(z == 1)
    def _():
        with scope("barwait"):
            greet()

    send_sums(0, first)

    @pl.when(z == 0)
    def _():
        for d in range(nt):
            far(d, 0, 0, 1).start()

    @pl.when(z == 2)
    def _():
        for d in range(nt):
            far(d, 1, 0, 1).start()

    @pl.when(z == 3)
    def _():
        for d in range(nt):
            far(d, 2, 0, 1).start()
        for d in range(nt):
            far(d, 2, 1, 2).start()

    with scope("g1"):
        @pl.loop(0, nc)
        def _(c):
            acc = product(nc + c)

            @pl.when(z == 0)
            def _():
                keep_value(acc, c)
                v_copy(c, 0, 1).start()

            @pl.when(z > 0)
            def _():
                finish(acc, second, c)

            @pl.when(z == 2)
            def _():
                q_copy(c, 0, 1, 1).start()

            @pl.when(z == 3)
            def _():
                q_copy(c, 0, 1, 2).start()

    @pl.when(z > 0)
    def _():
        send_sums(1, second)

    def near_scale(g):
        tot = sums_out[g]
        for d in range(1, nt):
            near(g, d).wait_recv()
            tot = tot + sums_in[g, d - 1]
        return lax.rsqrt(tot / width + 1e-06)

    def far_scale(slot):
        tot = None
        for d in range(nt):
            far(d, slot, 0, z).wait_recv()
            tot = sums_far[slot, d] if d == 0 else tot + sums_far[slot, d]
        return lax.rsqrt(tot / width + 1e-06)

    def set_rq(s, r):
        rqs[s] = jnp.transpose(jnp.broadcast_to(r[0:1, :] * HEAD_DIM ** (-0.5), (rows, rows)))

    def set_rk(r0, r1):
        left = lax.broadcasted_iota(jnp.int32, r0.shape, 1) < tok
        rks[0] = jnp.where(left, r0, pltpu.roll(r1, tok, 1))
        rks[1] = jnp.where(left, pltpu.roll(r0, tok, 1), r1)

    lane = lax.broadcasted_iota(jnp.int32, (tok, HEAD_DIM), 1)

    def attend(c, js, lo, hi, nk, merged):
        row = lax.broadcasted_iota(jnp.int32, (tok, nk * tok), 0)
        col = lax.broadcasted_iota(jnp.int32, (tok, nk * tok), 1)
        allowed = (col <= row) | (col >= tok)
        units = [(j, h, slice(h * HEAD_DIM, (h + 1) * HEAD_DIM)) for j in js for h in range(2)]
        spans = range(lo, hi)
        scores = [
            lax.dot_general(
                qk[1, c, j, lo * tok : hi * tok, hs], qk[0, c, j, 0 : nk * tok, hs],
                (((1,), (1,)), ((), ())), preferred_element_type=F32,
            )
            for j, h, hs in units
        ]
        scaled = []
        for (j, h, hs), score in zip(units, scores):
            for s in spans:
                sc = score[(s - lo) * tok : (s - lo + 1) * tok]
                sc = sc * rqs[s, j * tok : (j + 1) * tok, 0 : nk * tok] * rks[j, 0:1, 0 : nk * tok]
                scaled.append(jnp.where(allowed, sc, -1e30) if s == 0 else sc)
        tops = [jnp.max(sc, axis=1, keepdims=True) for sc in scaled]
        expos = [jnp.exp(sc - top) for sc, top in zip(scaled, tops)]
        tots = [jnp.sum(e, axis=1, keepdims=True) for e in expos]
        n = hi - lo
        accs = []
        for i, (j, h, hs) in enumerate(units):
            w = [e.astype(BF16) for e in expos[i * n : (i + 1) * n]]
            w = w[0] if n == 1 else jnp.concatenate(w, axis=0)
            accs.append(jnp.dot(w, vbuf[c, j, 0 : nk * tok, hs], preferred_element_type=F32))
        for i, (j, h, hs) in enumerate(units):
            for s in spans:
                o = accs[i][(s - lo) * tok : (s - lo + 1) * tok] / tots[i * n + s - lo]
                if s == 0 and not merged:
                    mixed[j * tok : (j + 1) * tok, pl.ds(pl.multiple_of(c * COLS + h * HEAD_DIM, HEAD_DIM), HEAD_DIM)] = o.astype(BF16)
                elif s == 0:
                    own_o[c, j, :, hs] = o
                else:
                    oout[s - 1, c, j, :, hs] = o.astype(BF16)
        if not merged:
            return
        for i, j in enumerate(js):
            for s in spans:
                a, b = (tops[u] + jnp.log(tots[u]) for u in (2 * i * n + s - lo, (2 * i + 1) * n + s - lo))
                if s > 0:
                    lse_out[j, s - 1] = jnp.where(lane == 2 * c, a, jnp.where(lane == 2 * c + 1, b, lse_out[j, s - 1]))
                else:
                    own_lse[j] = jnp.where(lane == 2 * c, a, jnp.where(lane == 2 * c + 1, b, own_lse[j]))

    def remote_part(c, j):
        @pl.when(z == 1)
        def _():
            with scope("attwait"):
                q_copy(c, j, 1, z).wait_recv()
                q_copy(c, j, 2, z).wait_recv()
                if j == 0:
                    k_copy(c, 0, z).wait_recv()
                    v_copy(c, 0, z).wait_recv()
            attend(c, (j,), 1, 3, 2, True)
            o_copy(c, j, 1, 2).start()
            o_copy(c, j, 2, 3).start()

        @pl.when(z == 2)
        def _():
            with scope("attwait"):
                q_copy(c, j, 1, z).wait_recv()
            attend(c, (j,), 0, 2, 1, True)
            o_copy(c, j, 1, 3).start()

    def send_lse(j):
        def message(a, b):
            lse_msg[j] = jnp.transpose(jnp.concatenate([a, b], axis=0))[0:16]

        @pl.when(z == 1)
        def _():
            message(lse_out[j, 0], lse_out[j, 1])
            l_copy(j, 1, 2).start()
            l_copy(j, 2, 3).start()

        @pl.when(z == 2)
        def _():
            message(lse_out[j, 0], lse_out[j, 0])
            l_copy(j, 1, 3).start()

    with scope("g2"):
        @pl.loop(0, nc)
        def _(c):
            acc = product(2 * nc + c)

            @pl.when(z == 0)
            def _():
                finish(acc, 1, c)
                k_copy(c, 1, 1).start()
                v_copy(c, 1, 1).start()

            @pl.when(z > 0)
            def _():
                keep_value(acc, c)

            @pl.when(z == 2)
            def _():
                q_copy(c, 1, 1, 1).start()

            @pl.when(z == 3)
            def _():
                q_copy(c, 1, 2, 1).start()
                q_copy(c, 1, 1, 2).start()

            @pl.when((c == 0) & (z == 1))
            def _():
                with scope("sumwait"):
                    set_rk(near_scale(0), far_scale(0))
                    set_rq(0, near_scale(1))
                    set_rq(1, far_scale(1))
                    set_rq(2, far_scale(2))

            @pl.when((c == 0) & high)
            def _():
                with scope("sumwait"):
                    set_rq(0, near_scale(0))
                    r = near_scale(1)
                    set_rk(r, r)

            @pl.when((c == 0) & (z == 2))
            def _():
                with scope("sumwait"):
                    set_rq(1, far_scale(2))

            remote_part(c, 0)

            @pl.when(z == 3)
            def _():
                attend(c, (0, 1), 0, 1, 1, True)

    send_lse(0)

    @pl.when(z == 0)
    def _():
        with scope("own"):
            send_sums(1, 1)
            r = near_scale(0)
            set_rk(r, r)
            set_rq(0, near_scale(1))

            @pl.loop(0, nc)
            def _(c):
                attend(c, (0, 1), 0, 1, 1, False)

    @pl.when(z == 1)
    def _():
        with scope("own"):
            @pl.loop(0, nc)
            def _(c):
                k_copy(c, 1, z).wait_recv()
                v_copy(c, 1, z).wait_recv()
                attend(c, (0, 1), 0, 1, 2, False)

    with scope("rem1"):
        @pl.when((z == 1) | (z == 2))
        def _():
            @pl.loop(0, nc)
            def _(c):
                remote_part(c, 1)

        send_lse(1)

    def merge(j, ni):
        lses = [own_lse[j]]
        for s in range(1, ni + 1):
            l_copy(j, s, z).wait_recv()
            wide = jnp.concatenate([lse_in[s - 1, j], jnp.zeros((rows - 16, rows), F32)], axis=0)
            lses.append(jnp.transpose(wide)[(ni - 1) * tok : ni * tok])
        top = functools.reduce(jnp.maximum, lses)
        parts = [jnp.exp(v - top) for v in lses]
        tot = functools.reduce(jnp.add, parts)
        for s in range(ni + 1):
            shares[s] = parts[s] / tot

        @pl.loop(0, nc)
        def _(c):
            for s in range(1, ni + 1):
                o_copy(c, j, s, z).wait_recv()
            for h in range(2):
                hs = slice(h * HEAD_DIM, (h + 1) * HEAD_DIM)
                o = 0.0
                for s in range(ni + 1):
                    share = jnp.sum(jnp.where(lane == 2 * c + h, shares[s], 0.0), axis=1, keepdims=True)
                    o += share * (own_o[c, j, :, hs] if s == 0 else oin[s - 1, c, j, :, hs].astype(F32))
                mixed[j * tok : (j + 1) * tok, pl.ds(pl.multiple_of(c * COLS + h * HEAD_DIM, HEAD_DIM), HEAD_DIM)] = o.astype(BF16)

    share = tok // nt

    def rs_copy(n, j, d):
        to = lax.rem(me + d, nt)
        return remote(
            part.at[n, j, pl.ds(pl.multiple_of(to * share, share), share)], rs_in.at[d - 1, n, j],
            rs_send.at[d - 1, j, n], rs_recv.at[d - 1, j, n], (dp, z, to),
        )

    for j in range(2):
        with scope("merge"):
            @pl.when(z == 2)
            def _():
                merge(j, 1)

            @pl.when(z == 3)
            def _():
                merge(j, 2)

        with scope("outp"):
            @pl.loop(0, no)
            def _(n):
                if j == 0:
                    wo_copy(n).wait()
                acc = jnp.dot(mixed[j * tok : (j + 1) * tok], wov[n], preferred_element_type=F32)
                part[n, j] = acc.astype(BF16)
                for d in range(1, nt):
                    rs_copy(n, j, d).start()

    with scope("rs"):
        for j in range(2):

            @pl.loop(0, no)
            def _(n):
                for d in range(1, nt):
                    rs_copy(n, j, d).wait_recv()
                o = part[n, j, pl.ds(pl.multiple_of(me * share, share), share)].astype(F32)
                for d in range(1, nt):
                    o += rs_in[d - 1, n, j].astype(F32)
                out_ref[:, j, pl.ds(pl.multiple_of(n * oc, oc), oc)] = o.astype(BF16)

    for j in range(2):

        @pl.loop(0, no)
        def _(n):
            for d in range(1, nt):
                rs_copy(n, j, d).wait_send()

    _t = scope("tail")
    _t.__enter__()
    for g in range(2):
        for d in range(1, nt):
            near(g, d).wait_send()

    @pl.when(z == 0)
    def _():
        for d in range(nt):
            far(d, 0, 0, 1).wait_send()

        @pl.loop(0, nc)
        def _(c):
            for j in range(2):
                k_copy(c, j, 1).wait_send()
                v_copy(c, j, 1).wait_send()

    @pl.when(z == 1)
    def _():
        for j in range(2):
            l_copy(j, 1, 2).wait_send()
            l_copy(j, 2, 3).wait_send()

            @pl.loop(0, nc)
            def _(c):
                o_copy(c, j, 1, 2).wait_send()
                o_copy(c, j, 2, 3).wait_send()

    @pl.when(z == 2)
    def _():
        for d in range(nt):
            far(d, 1, 0, 1).wait_send()
        for j in range(2):
            l_copy(j, 1, 3).wait_send()

            @pl.loop(0, nc)
            def _(c):
                q_copy(c, j, 1, 1).wait_send()
                o_copy(c, j, 1, 3).wait_send()

    @pl.when(z == 3)
    def _():
        for d in range(nt):
            far(d, 2, 0, 1).wait_send()
            far(d, 2, 1, 2).wait_send()
        for j in range(2):

            @pl.loop(0, nc)
            def _(c):
                q_copy(c, j, 2, 1).wait_send()
                q_copy(c, j, 1, 2).wait_send()

    _t.__exit__(None, None, None)


def fused(ns, nt, tokens, w_query, w_key, w_value, w_out, gain_query, gain_key):
    tok, seqs, depth = tokens.shape
    local = w_query.shape[1]
    nc = local // COLS
    oc = 1024
    no = depth // oc
    rows = tok * seqs
    width = HEADS * HEAD_DIM
    vm = pltpu.VMEM
    dma = pltpu.SemaphoreType.DMA
    scratch = [
        vm((RING, depth, COLS), BF16), vm((no, local, oc), BF16),
        vm((tok, seqs, depth), BF16), vm((rows, depth), BF16), vm((rows, depth), BF16),
        vm((rows, HEAD_DIM), F32), vm((rows, HEAD_DIM), F32), vm((2, nc, 1, COLS), F32), vm((2, rows, HEAD_DIM), F32),
        vm((2, 8, rows), F32), vm((2, nt - 1, 8, rows), F32), vm((3, nt, 8, rows), F32),
        vm((3, rows, rows), F32), vm((2, 8, rows), F32),
        vm((2, nc, seqs, 3 * tok, COLS), BF16), vm((nc, seqs, 2 * tok, COLS), BF16),
        vm((nc, seqs, tok, COLS), F32), vm((seqs, tok, HEAD_DIM), F32),
        vm((2, nc, seqs, tok, COLS), BF16), vm((seqs, 2, tok, HEAD_DIM), F32), vm((seqs, 16, rows), F32),
        vm((2, nc, seqs, tok, COLS), BF16), vm((2, seqs, 16, rows), F32), vm((3, tok, HEAD_DIM), F32),
        vm((rows, local), BF16), vm((no, seqs, tok, oc), BF16), vm((nt - 1, no, seqs, tok // nt, oc), BF16),
        dma, dma((RING,)), dma((no,)), dma((2, nt - 1)), dma((2, nt - 1)), dma((2, nt)), dma((3, nt)),
        dma((2, nc)), dma((2, nc)), dma((2, nc)), dma((2, nc)),
        dma((2, 2, nc)), dma((2, 2, nc)), dma((2, 2, nc)), dma((2, 2, nc)), dma((2, 2)), dma((2, 2)),
        dma((nt - 1, 2, no)), dma((nt - 1, 2, no)),
    ]
    in_vmem = pl.BlockSpec(memory_space=pltpu.VMEM)
    anywhere = pl.BlockSpec(memory_space=pl.ANY)
    return pl.pallas_call(
        functools.partial(block_kernel, ns, nt, tok, width),
        out_shape=jax.ShapeDtypeStruct((tok // nt, seqs, depth), BF16),
        in_specs=[anywhere] + [in_vmem] * 2 + [anywhere] * 4,
        out_specs=in_vmem,
        scratch_shapes=scratch,
        compiler_params=pltpu.CompilerParams(collective_id=0, has_side_effects=True, vmem_limit_bytes=60 * 1024 * 1024),
    )(tokens, gain_query, gain_key, w_query, w_key, w_value, w_out)


def rotary(field, positions):
    half = HEAD_DIM // 2
    shaped = field.reshape(field.shape[0], -1, HEAD_DIM)
    freqs = jnp.exp(-jnp.log(500000.0) * jnp.arange(half, dtype=jnp.float32) * 2.0 / HEAD_DIM)
    angle = positions.astype(jnp.float32)[:, None] * freqs[None, :]
    cosine = jnp.cos(angle)[:, None, :]
    sine = jnp.sin(angle)[:, None, :]
    first = shaped[..., :half]
    second = shaped[..., half:]
    turned = jnp.concatenate(
        [first * cosine - second * sine, second * cosine + first * sine], axis=-1
    )
    return turned.reshape(field.shape[0], -1)


def local(tokens, w_query, w_key, w_value, w_out, gain_query, gain_key):
    tok_rows = tokens.shape[0]
    seq_count = tokens.shape[1]
    local_width = w_query.shape[1]
    local_heads = local_width // HEAD_DIM
    width = HEADS * HEAD_DIM
    flat = tokens.reshape(tok_rows * seq_count, tokens.shape[2])
    query = jnp.dot(flat, w_query, preferred_element_type=jnp.float32)
    key_raw = jnp.dot(flat, w_key, preferred_element_type=jnp.float32)
    sum_query, sum_key = lax.psum(
        (jnp.sum(query * query, axis=1), jnp.sum(key_raw * key_raw, axis=1)), "tensor"
    )
    value = jnp.dot(flat, w_value, preferred_element_type=jnp.float32).astype(jnp.bfloat16)
    scale_q = lax.rsqrt(sum_query / width + 1e-06)
    scale_k = lax.rsqrt(sum_key / width + 1e-06)
    my_block = lax.axis_index("seq")
    positions = my_block * tok_rows + jnp.arange(tok_rows, dtype=jnp.int32)
    row_positions = (positions[:, None] + jnp.zeros((1, seq_count), jnp.int32)).reshape(-1)
    q_normed = rotary(query * scale_q[:, None] * gain_query[None, :], row_positions).astype(
        jnp.bfloat16
    )
    k_normed = rotary(key_raw * scale_k[:, None] * gain_key[None, :], row_positions).astype(
        jnp.bfloat16
    )
    q_heads = q_normed.reshape(tok_rows, seq_count, local_heads, HEAD_DIM)
    k_local = k_normed.reshape(tok_rows, seq_count, local_width)
    v_local = value.reshape(tok_rows, seq_count, local_width)
    factor = HEAD_DIM ** (-0.5)
    piece = (
        lax.all_gather(k_local, "seq", axis=0, tiled=True),
        lax.all_gather(v_local, "seq", axis=0, tiled=True),
    )
    key_pos = jnp.arange(piece[0].shape[0], dtype=jnp.int32)
    key_block = piece[0]
    count = key_block.shape[0]
    key_heads = key_block.reshape(count, seq_count, local_heads, HEAD_DIM)
    value_heads = piece[1].reshape(count, seq_count, local_heads, HEAD_DIM)
    scores = (
        jnp.einsum("qshd,kshd->shqk", q_heads, key_heads, preferred_element_type=jnp.float32)
        * factor
    )
    allowed = (key_pos[None, None, None, :] <= positions[None, None, :, None]) & (
        key_pos[None, None, None, :] >= 0
    )
    old_max = jnp.full((seq_count, local_heads, tok_rows), -1e30, jnp.float32)
    new_max = jnp.maximum(old_max, jnp.max(jnp.where(allowed, scores, -1e30), axis=3))
    expo = jnp.where(allowed, jnp.exp(scores - new_max[..., None]), 0.0)
    new_total = jnp.sum(expo, axis=3)
    added = jnp.einsum(
        "shqk,kshd->shqd",
        expo.astype(jnp.bfloat16),
        value_heads,
        preferred_element_type=jnp.float32,
    )
    final_state = (new_max, new_total, added)
    final_max, final_total, final_acc = final_state
    mixed = (final_acc / final_total[..., None]).astype(jnp.bfloat16)
    mixed = jnp.transpose(mixed, (2, 0, 1, 3)).reshape(tok_rows, seq_count, local_width)
    return lax.psum_scatter(
        jnp.dot(mixed, w_out, preferred_element_type=jnp.float32).astype(jnp.bfloat16),
        "tensor",
        scatter_dimension=0,
        tiled=True,
    )


def solution(mesh):
    ns, nt = mesh.shape["seq"], mesh.shape["tensor"]
    step = functools.partial(fused, ns, nt) if ns == 4 and nt == 4 else local
    return jax.shard_map(
        step,
        mesh=mesh,
        in_specs=(
            P("seq", "dp", None),
            P(None, "tensor"),
            P(None, "tensor"),
            P(None, "tensor"),
            P("tensor", None),
            P("tensor"),
            P("tensor"),
        ),
        out_specs=P(("seq", "tensor"), "dp", None),
        check_vma=False,
    )
```

time: 65.2 us -> 45 us (0.69)
  Pallas kernels: 60.4 us -> 42.8 us
  local copies, waits for them, and re-layouts: 4.67 us -> 1.92 us
    pallas_call x1, Pallas kernels: 60.4 us -> 42.8 us  [fused(): pl.pallas_call(functools.partial(block_kernel, ns, nt, tok, width), out_s...]
    transpose x2 -> x0, local copies, waits for them, and re-layouts: 4.67 us -> none  [the longest x1 2.63 us: fused(): x = jnp.transpose(tokens, (1, 0, 2)).reshape(rows, depth)]
    unnamed x0 -> x1, local copies, waits for them, and re-layouts: none -> 1.92 us
where the time goes in v1:
time: 45 us; the launch traced here: 44.8 us
  Pallas kernels  42.8 us (95%)
  local copies, waits for them, and re-layouts  1.92 us (4%)
    pallas_call x1, Pallas kernels, fused(): pl.pallas_call(functools.partial(block_kernel, ns, nt, tok, width), out_s...  42.8 us
    unnamed x1, local copies, waits for them, and re-layouts  1.92 us

profile of v1, /device:TPU:24, one launch (start us, length us, event | category | flops | bytes accessed | tf_op | source)
XLA Modules:
  0.0 44.8 jit_solution(8425356921939617707)
XLA Ops:
  0.0 42.8 %shard_map.73 = bf16[16,2,5120]{2,1,0:T(2,128)(2,1)} custom-call(bf16[64,2,5120]{2,1,0:T(2,128)(2,1)} %x_hbm.1, f32[1280]{0:T(1024)} %gq_in.1, f32[1280]{0:T(1024)} %gk_in.1, bf16[5120,1280]{1,0:T(8,128)(2,1)} %wq.1, bf16[5120,1280]{1,0:T(8,128)(2,1)} %wk.1, bf16[5120,1280]{1,0:T(8,128)(2,1)} %wv.1, bf16[1280,5120]{1,0:T(8,128)(2,1)} %wo.1), custom_call_target="tpu_custom_call" | custom-call | tf_op jit(solution)/shard_map/pallas_call | solution.py:606
  42.9 1.9 %copy.9 = bf16[16,2,5120]{2,1,0:T(2,128)(2,1)} copy(bf16[16,2,5120]{2,1,0:T(2,128)(2,1)} %shard_map.73) | data formatting | bytes 655360

commit v2 on v1

v2 whole, which is shorter than its diff:
```python
import contextlib
import functools

import jax
import jax.numpy as jnp
from jax import lax
from jax.experimental import pallas as pl
from jax.experimental.pallas import tpu as pltpu
from jax.sharding import PartitionSpec as P

HEADS = 40
HEAD_DIM = 128
MESH = pl.DeviceIdType.MESH
COLS = 2 * HEAD_DIM
RING = 9
LIFT = 1
F32 = jnp.float32
BF16 = jnp.bfloat16


def scope(name):
    return contextlib.nullcontext()


def block_kernel(
    ns, nt, tok, width,
    x_hbm, gq_hbm, gk_hbm, wq, wk, wv, wo,
    out_ref,
    gq_in, gk_in, ring, wov, xin, xi, xs, cos_ref, sin_ref, gains, ssq,
    sums_out, sums_in, sums_far, rqs, rks,
    qk, vbuf, own_o, own_lse, oout, lse_out, lse_msg, oin, lse_in, shares,
    mixed, part, rs_one, rs_mid, rs_two,
    x_sem, g_sem, w_sem, wo_sem, sum_send, sum_recv, far_send, far_recv, k_send, v_send, kv_recv,
    q_send, q_recv, o_send, o_recv, l_send, l_recv, one_send, one_recv, two_send, two_recv,
):
    dp = lax.axis_index("dp")
    z = lax.axis_index("seq")
    me = lax.axis_index("tensor")
    low = z < 2
    high = z >= 2
    nc = vbuf.shape[0]
    rows = 2 * tok
    oc = wov.shape[2]
    no = wov.shape[0]

    def w_copy(ref, c, slot):
        return pltpu.make_async_copy(
            ref.at[:, pl.ds(pl.multiple_of(c * COLS, COLS), COLS)], ring.at[slot], w_sem.at[slot]
        )

    def wo_copy(c):
        return pltpu.make_async_copy(
            wo.at[:, pl.ds(pl.multiple_of(c * oc, oc), oc)], wov.at[c], wo_sem.at[c]
        )

    def start(i):
        slot = lax.rem(i, RING)
        group = i // nc
        c = i - group * nc
        inside = i < 3 * nc

        @pl.when(inside & ((low & (group == 0)) | (high & (group == 1))))
        def _():
            w_copy(wk, c, slot).start()

        @pl.when(inside & ((low & (group == 1)) | (high & (group == 2))))
        def _():
            w_copy(wv, c, slot).start()

        @pl.when(inside & ((low & (group == 2)) | (high & (group == 0))))
        def _():
            w_copy(wq, c, slot).start()

        @pl.when((i >= 3 * nc) & (i < 3 * nc + no))
        def _():
            wo_copy(i - 3 * nc).start()

    x_copy = pltpu.make_async_copy(x_hbm, xin, x_sem)
    x_copy.start()
    g_copies = [pltpu.make_async_copy(gk_hbm, gk_in, g_sem.at[0]), pltpu.make_async_copy(gq_hbm, gq_in, g_sem.at[1])]
    for copy in g_copies:
        copy.start()

    barrier = pltpu.get_barrier_semaphore()
    linked = {0: (1, 2), 1: (0, 2, 3), 2: (0, 1, 3), 3: (1, 2)}
    for d in range(1, nt):
        pl.semaphore_signal(barrier, inc=1, device_id=(dp, z, lax.rem(me + d, nt)), device_id_type=MESH)
    for a in range(ns):
        hit = functools.reduce(jnp.logical_or, [z == b for b in linked[a]])

        @pl.when(hit)
        def _():
            for d in range(nt):
                pl.semaphore_signal(barrier, inc=1, device_id=(dp, a, lax.rem(me + d, nt)), device_id_type=MESH)

    def greet():
        pl.semaphore_wait(barrier, nt - 1 + nt * jnp.where((z == 1) | (z == 2), 3, 2))

    def remote(src, dst, ssem, rsem, to):
        return pltpu.make_async_remote_copy(
            src_ref=src, dst_ref=dst, send_sem=ssem, recv_sem=rsem, device_id=to, device_id_type=MESH
        )

    def settle(ref, sem):
        pltpu.make_async_copy(ref, ref, sem).wait()

    def k_copy(c, j, b, to):
        at = b * tok
        return remote(qk.at[0, c, j, pl.ds(0, tok)], qk.at[0, c, j, pl.ds(at, tok)], k_send.at[to - 1], kv_recv.at[j, c], (dp, to, me))

    def v_copy(c, j, b, to):
        at = b * tok
        return remote(vbuf.at[c, j, pl.ds(0, tok)], vbuf.at[c, j, pl.ds(at, tok)], v_send.at[to - 1], kv_recv.at[j, c], (dp, to, me))

    def q_copy(c, j, s, to):
        return remote(qk.at[1, c, j, pl.ds(0, tok)], qk.at[1, c, j, pl.ds(s * tok, tok)], q_send.at[s - 1], q_recv.at[j, c], (dp, to, me))

    def o_copy(c, j, s, to):
        return remote(oout.at[s - 1, c, j], oin.at[s - 1, c, j], o_send.at[s - 1], o_recv.at[j, c], (dp, to, me))

    def l_copy(j, s, to):
        return remote(lse_msg.at[j], lse_in.at[s - 1, j], l_send.at[s - 1], l_recv.at[j], (dp, to, me))

    def near(g, d):
        return remote(sums_out.at[g], sums_in.at[g, d - 1], sum_send.at[g], sum_recv.at[g], (dp, z, lax.rem(me + d, nt)))

    def far(d, slot, ss, to):
        return remote(sums_out.at[0], sums_far.at[slot, d], far_send.at[ss], far_recv.at[slot], (dp, to, lax.rem(me + d, nt)))

    def product(i):
        slot = lax.rem(i, RING)
        start(i + RING - 1)
        with scope("wwait"):
            w_copy(wk, 0, slot).wait()
        return jnp.dot(xs[...], ring[slot], preferred_element_type=F32)

    def turned(acc, kind, c):
        cosine, sine = cos_ref[...], sin_ref[...]
        for h in range(2):
            y = acc[:, h * HEAD_DIM : (h + 1) * HEAD_DIM] * gains[kind, c, :, h * HEAD_DIM : (h + 1) * HEAD_DIM]
            y = (y * cosine + pltpu.roll(y, HEAD_DIM // 2, 1) * sine).astype(BF16)
            for j in range(2):
                qk[kind, c, j, 0:tok, h * HEAD_DIM : (h + 1) * HEAD_DIM] = y[j * tok : (j + 1) * tok]

    def finish(acc, kind, c):
        ssq[kind] += acc[:, :HEAD_DIM] * acc[:, :HEAD_DIM] + acc[:, HEAD_DIM:] * acc[:, HEAD_DIM:]
        turned(acc, kind, c)

    def keep_value(acc, c):
        v = acc.astype(BF16)
        for j in range(2):
            vbuf[c, j, 0:tok, :] = v[j * tok : (j + 1) * tok]

    with scope("init"):
        lanes = lax.broadcasted_iota(jnp.int32, (tok, HEAD_DIM), 1)
        half = HEAD_DIM // 2
        freqs = jnp.exp(-jnp.log(500000.0) * lax.rem(lanes, half).astype(F32) * 2.0 / HEAD_DIM)
        spot = z * tok + lax.broadcasted_iota(jnp.int32, (tok, HEAD_DIM), 0)
        angle = spot.astype(F32) * freqs
        cosine = jnp.cos(angle)
        sine = jnp.sin(angle)
        sine = jnp.where(lanes < half, -sine, sine)
        for j in range(2):
            cos_ref[j * tok : (j + 1) * tok] = cosine
            sin_ref[j * tok : (j + 1) * tok] = sine

        @pl.loop(0, RING - 1)
        def _(i):
            start(i)

        for copy in g_copies:
            copy.wait()
        for c in range(nc):
            gains[0, c] = gk_in[c * COLS : (c + 1) * COLS].reshape(1, COLS)
            gains[1, c] = gq_in[c * COLS : (c + 1) * COLS].reshape(1, COLS)
        ssq[...] = jnp.zeros_like(ssq)
        sums_out[...] = jnp.zeros_like(sums_out)
        own_lse[...] = jnp.zeros_like(own_lse)
        lse_out[...] = jnp.full_like(lse_out, -1e30)

    with scope("xwait"):
        x_copy.wait()
    with scope("xlay"):
        @pl.loop(0, tok // 8)
        def _(i):
            v = xin[pl.ds(pl.multiple_of(i * 8, 8), 8)]
            xi[pl.ds(pl.multiple_of(i * 16, 16), 16), :] = v.reshape(16, v.shape[-1])

        r = lax.broadcasted_iota(jnp.int32, (rows, rows), 0)
        q = lax.broadcasted_iota(jnp.int32, (rows, rows), 1)
        pick = (q == jnp.where(r < tok, 2 * r, 2 * (r - tok) + 1)).astype(F32).astype(BF16)

        half_depth = xs.shape[1] // 2
        for i in range(2):
            at = slice(i * half_depth, (i + 1) * half_depth)
            xs[:, at] = jnp.dot(pick, xi[:, at], preferred_element_type=F32).astype(BF16)

    def fill_sums(g, kind):
        sums_out[g, 0:1, :] = jnp.sum(jnp.transpose(ssq[kind]), axis=0, keepdims=True)

    def send_near(g):
        for d in range(1, nt):
            near(g, d).start()

    def send_sums(g, kind):
        fill_sums(g, kind)
        send_near(g)

    first = jnp.where(low, 0, 1)

    with scope("g0"):
        @pl.loop(0, nc)
        def _(c):
            acc = product(c)

            @pl.when((c == 0) & ((z == 0) | (z == 3)))
            def _():
                greet()

            finish(acc, first, c)

            @pl.when((z == 0) & (c < LIFT))
            def _():
                k_copy(c, 0, 1, 2).start()

            @pl.when((z == 0) & (c >= LIFT))
            def _():
                k_copy(c, 0, 1, 1).start()

            @pl.when((z == 3) & (c < LIFT))
            def _():
                q_copy(c, 0, 1, 2).start()

            @pl.when((z == 3) & (c >= LIFT) & (c < nc - 2))
            def _():
                q_copy(c, 0, 2, 1).start()

    @pl.when((z == 1) | (z == 2))
    def _():
        with scope("barwait"):
            greet()

    fill_sums(0, first)

    @pl.when(z == 0)
    def _():
        for to in (1, 2):
            for d in range(nt):
                far(d, 0, to - 1, to).start()

    @pl.when(z == 1)
    def _():
        for d in range(nt):
            far(d, 1, 0, 2).start()

    @pl.when(z == 2)
    def _():
        for d in range(nt):
            far(d, 1, 0, 1).start()

    @pl.when(z == 3)
    def _():
        for to in (1, 2):
            for d in range(nt):
                far(d, 2, to - 1, to).start()

    send_near(0)

    @pl.when(z == 3)
    def _():
        @pl.loop(nc - 2, nc)
        def _(c):
            q_copy(c, 0, 2, 1).start()

    @pl.when(z == 1)
    def _():
        @pl.loop(0, LIFT)
        def _(c):
            for j in range(2):
                k_copy(c, j, 2, 2).start()

    with scope("g1"):
        @pl.loop(0, nc)
        def _(c):
            acc = product(nc + c)

            @pl.when(low)
            def _():
                keep_value(acc, c)

            @pl.when(high)
            def _():
                finish(acc, 0, c)

            @pl.when((z == 0) & (c < LIFT))
            def _():
                v_copy(c, 0, 1, 2).start()

            @pl.when((z == 0) & (c >= LIFT))
            def _():
                v_copy(c, 0, 1, 1).start()

            @pl.when((z == 1) & (c < LIFT))
            def _():
                for j in range(2):
                    v_copy(c, j, 2, 2).start()

            @pl.when((z == 2) & (c >= LIFT))
            def _():
                q_copy(c, 0, 1, 1).start()

            @pl.when((z == 3) & (c >= LIFT))
            def _():
                q_copy(c, 0, 1, 2).start()

            @pl.when((z == 3) & (c < LIFT))
            def _():
                q_copy(c, 1, 1, 2).start()

    @pl.when(high)
    def _():
        send_sums(1, 0)

    def near_scale(g):
        settle(sums_in.at[g], sum_recv.at[g])
        tot = sums_out[g]
        for d in range(1, nt):
            tot = tot + sums_in[g, d - 1]
        return lax.rsqrt(tot / width + 1e-06)

    def far_scale(slot):
        settle(sums_far.at[slot], far_recv.at[slot])
        tot = sums_far[slot, 0]
        for d in range(1, nt):
            tot = tot + sums_far[slot, d]
        return lax.rsqrt(tot / width + 1e-06)

    def set_rq(s, r):
        rqs[s] = jnp.transpose(jnp.broadcast_to(r[0:1, :] * HEAD_DIM ** (-0.5), (2 * rows, rows)))

    def set_rk(r0, r1, r2=None):
        left = lax.broadcasted_iota(jnp.int32, r0.shape, 1) < tok
        rks[0, :, 0:rows] = jnp.where(left, r0, pltpu.roll(r1, tok, 1))
        rks[1, :, 0:rows] = jnp.where(left, pltpu.roll(r0, tok, 1), r1)
        if r2 is not None:
            rks[0, :, rows : 2 * rows] = r2
            rks[1, :, rows : 2 * rows] = pltpu.roll(r2, tok, 1)

    lane = lax.broadcasted_iota(jnp.int32, (tok, HEAD_DIM), 1)

    def attend(c, js, lo, hi, nk, whole):
        row = lax.broadcasted_iota(jnp.int32, (tok, nk * tok), 0)
        col = lax.broadcasted_iota(jnp.int32, (tok, nk * tok), 1)
        allowed = (col <= row) | (col >= tok)
        units = [(j, h, slice(h * HEAD_DIM, (h + 1) * HEAD_DIM)) for j in js for h in range(2)]
        spans = range(lo, hi)
        scores = [
            lax.dot_general(
                qk[1, c, j, lo * tok : hi * tok, hs], qk[0, c, j, 0 : nk * tok, hs],
                (((1,), (1,)), ((), ())), preferred_element_type=F32,
            )
            for j, h, hs in units
        ]
        scaled = []
        for (j, h, hs), score in zip(units, scores):
            for s in spans:
                sc = score[(s - lo) * tok : (s - lo + 1) * tok]
                sc = sc * rqs[s, j * tok : (j + 1) * tok, 0 : nk * tok] * rks[j, 0:1, 0 : nk * tok]
                scaled.append(jnp.where(allowed, sc, -1e30) if s == 0 else sc)
        tops = [jnp.max(sc, axis=1, keepdims=True) for sc in scaled]
        expos = [jnp.exp(sc - top) for sc, top in zip(scaled, tops)]
        tots = [jnp.sum(e, axis=1, keepdims=True) for e in expos]
        n = hi - lo
        accs = []
        for i, (j, h, hs) in enumerate(units):
            w = [e.astype(BF16) for e in expos[i * n : (i + 1) * n]]
            w = w[0] if n == 1 else jnp.concatenate(w, axis=0)
            accs.append(jnp.dot(w, vbuf[c, j, 0 : nk * tok, hs], preferred_element_type=F32))
        for i, (j, h, hs) in enumerate(units):
            for s in spans:
                o = accs[i][(s - lo) * tok : (s - lo + 1) * tok] / tots[i * n + s - lo]
                if s == 0 and whole:
                    mixed[j * tok : (j + 1) * tok, pl.ds(pl.multiple_of(c * COLS + h * HEAD_DIM, HEAD_DIM), HEAD_DIM)] = o.astype(BF16)
                elif s == 0:
                    own_o[c, j, :, hs] = o
                else:
                    oout[s - 1, c, j, :, hs] = o.astype(BF16)
        for i, j in enumerate(js):
            for s in spans:
                if s == 0 and whole:
                    continue
                a, b = (tops[u] + jnp.log(tots[u]) for u in (2 * i * n + s - lo, (2 * i + 1) * n + s - lo))
                if s > 0:
                    lse_out[j, s - 1] = jnp.where(lane == 2 * c, a, jnp.where(lane == 2 * c + 1, b, lse_out[j, s - 1]))
                else:
                    own_lse[j] = jnp.where(lane == 2 * c, a, jnp.where(lane == 2 * c + 1, b, own_lse[j]))

    def remote_part(c, j):
        @pl.when(z == 1)
        def _():
            with scope("attwait"):
                settle(qk.at[1, c, :, pl.ds(0, tok)], q_recv.at[j, c])
                settle(qk.at[0, c, :, pl.ds(0, tok)], kv_recv.at[j, c])
            attend(c, (j,), 1, 3, 2, False)
            o_copy(c, j, 2, 3).start()
            o_copy(c, j, 1, 2).start()

        @pl.when(z == 2)
        def _():
            with scope("attwait"):
                settle(qk.at[1, c, j, pl.ds(0, tok)], q_recv.at[j, c])
            attend(c, (j,), 0, 2, 1, False)
            o_copy(c, j, 1, 3).start()

    def lifted_part(c, j):
        with scope("liftwait"):
            settle(qk.at[1, c, j, pl.ds(0, tok)], q_recv.at[j, c])
            settle(qk.at[0, c, :, pl.ds(0, 2 * tok)], kv_recv.at[j, c])
        attend(c, (j,), 0, 2, 3, True)
        o_copy(c, j, 1, 3).start()

    def send_lse(j):
        def message(a, b):
            lse_msg[j] = jnp.transpose(jnp.concatenate([a, b], axis=0))[0:16]

        @pl.when(z == 1)
        def _():
            message(lse_out[j, 0], lse_out[j, 1])
            l_copy(j, 2, 3).start()
            l_copy(j, 1, 2).start()

        @pl.when(z == 2)
        def _():
            message(lse_out[j, 0], lse_out[j, 0])
            l_copy(j, 1, 3).start()

    with scope("g2"):
        @pl.loop(0, nc)
        def _(c):
            acc = product(2 * nc + c)

            @pl.when(low)
            def _():
                finish(acc, 1, c)

            @pl.when(high)
            def _():
                keep_value(acc, c)

            @pl.when((z == 0) & (c >= LIFT))
            def _():
                k_copy(c, 1, 1, 1).start()
                v_copy(c, 1, 1, 1).start()

            @pl.when((z == 2) & (c >= LIFT))
            def _():
                q_copy(c, 1, 1, 1).start()

            @pl.when((z == 3) & (c >= LIFT))
            def _():
                q_copy(c, 1, 2, 1).start()
                q_copy(c, 1, 1, 2).start()

            @pl.when((c == LIFT) & (z == 1))
            def _():
                with scope("sw_near"):
                    a = near_scale(0)
                with scope("sw_far0"):
                    set_rk(a, far_scale(0))
                with scope("sw_far1"):
                    set_rq(1, far_scale(1))
                with scope("sw_far2"):
                    set_rq(2, far_scale(2))

            @pl.when((z == 1) & (c >= LIFT))
            def _():
                remote_part(c, 0)

    @pl.when(z == 0)
    def _():
        @pl.loop(0, LIFT)
        def _(c):
            k_copy(c, 1, 1, 2).start()
            v_copy(c, 1, 1, 2).start()

        @pl.loop(0, LIFT)
        def _(c):
            for j in range(2):
                k_copy(c, j, 1, 1).start()
                v_copy(c, j, 1, 1).start()

    @pl.when(low)
    def _():
        send_sums(1, 1)

    @pl.when(high)
    def _():
        with scope("sw_near"):
            set_rq(0, near_scale(0))
            r = near_scale(1)

        @pl.when(z == 3)
        def _():
            set_rk(r, r)

        @pl.when(z == 2)
        def _():
            with scope("sw_far"):
                set_rk(r, far_scale(0), far_scale(1))
                set_rq(1, far_scale(2))

    with scope("rem0"):
        @pl.when(z == 2)
        def _():
            @pl.loop(LIFT, nc)
            def _(c):
                remote_part(c, 0)

            @pl.loop(0, LIFT)
            def _(c):
                lifted_part(c, 0)

        send_lse(0)

    with scope("rem1"):
        @pl.when((z == 1) | (z == 2))
        def _():
            @pl.loop(LIFT, nc)
            def _(c):
                remote_part(c, 1)

        @pl.when(z == 2)
        def _():
            @pl.loop(0, LIFT)
            def _(c):
                lifted_part(c, 1)

        send_lse(1)

    @pl.when(z == 0)
    def _():
        with scope("own"):
            r = near_scale(0)
            set_rk(r, r)
            set_rq(0, near_scale(1))

            @pl.loop(0, nc)
            def _(c):
                attend(c, (0, 1), 0, 1, 1, True)

    @pl.when(z == 1)
    def _():
        with scope("own"):
            set_rq(0, near_scale(1))

            @pl.loop(0, nc)
            def _(i):
                c = lax.rem(i + LIFT, nc)

                @pl.when(c < LIFT)
                def _():
                    with scope("ownwait"):
                        for j in range(2):
                            settle(qk.at[0, c, :, pl.ds(0, tok)], kv_recv.at[j, c])

                attend(c, (0, 1), 0, 1, 2, True)

    @pl.when(z == 3)
    def _():
        with scope("own"):
            @pl.loop(0, nc)
            def _(c):
                attend(c, (0, 1), 0, 1, 1, False)

    def merge(j, ni):
        lses = [own_lse[j]]
        settle(lse_in.at[pl.ds(0, ni), j], l_recv.at[j])
        for s in range(1, ni + 1):
            wide = jnp.concatenate([lse_in[s - 1, j], jnp.zeros((rows - 16, rows), F32)], axis=0)
            lses.append(jnp.transpose(wide)[(ni - 1) * tok : ni * tok])
        top = functools.reduce(jnp.maximum, lses)
        parts = [jnp.exp(v - top) for v in lses]
        tot = functools.reduce(jnp.add, parts)
        for s in range(ni + 1):
            shares[s] = parts[s] / tot

        def blend(c, count):
            settle(oin.at[pl.ds(0, count), c, j], o_recv.at[j, c])
            for h in range(2):
                hs = slice(h * HEAD_DIM, (h + 1) * HEAD_DIM)
                o = 0.0
                for s in range(count + 1):
                    share = jnp.sum(jnp.where(lane == 2 * c + h, shares[s], 0.0), axis=1, keepdims=True)
                    o += share * (own_o[c, j, :, hs] if s == 0 else oin[s - 1, c, j, :, hs].astype(F32))
                mixed[j * tok : (j + 1) * tok, pl.ds(pl.multiple_of(c * COLS + h * HEAD_DIM, HEAD_DIM), HEAD_DIM)] = o.astype(BF16)

        if ni == 2:
            @pl.loop(0, LIFT)
            def _(c):
                blend(c, 1)

        @pl.loop(LIFT, nc)
        def _(c):
            blend(c, ni)

    share = tok // nt
    hc = oc // 2
    my, mx = me // 2, lax.rem(me, 2)

    def stage_one(n, j, half):
        if half == 0:
            src, to = part.at[n, j, half, :, 1 - mx], 2 * my + 1 - mx
        else:
            src, to = part.at[n, j, half, 1 - my], 2 * (1 - my) + mx
        return remote(src, rs_one.at[n, j, half], one_send, one_recv.at[j, n], (dp, z, to))

    def stage_two(n, j, half):
        to = 2 * (1 - my) + mx if half == 0 else 2 * my + 1 - mx
        return remote(rs_mid.at[n, j, half], rs_two.at[n, j, half], two_send, two_recv.at[j, n], (dp, z, to))

    def project(js, first_pass):
        lo, hi = js[0] * tok, (js[-1] + 1) * tok

        @pl.loop(0, no)
        def _(n):
            if first_pass:
                wo_copy(n).wait()
            acc = jnp.dot(mixed[lo:hi], wov[n], preferred_element_type=F32).astype(BF16)
            for j in js:
                for half in range(2):
                    for t in range(nt):
                        row = j * tok + t * share - lo
                        part[n, j, half, t // 2, t % 2] = acc[row : row + share, half * hc : (half + 1) * hc]
                    stage_one(n, j, half).start()

    def forward(j):
        with scope("fwd"):
            @pl.loop(0, no)
            def _(n):
                settle(rs_one.at[n, j], one_recv.at[j, n])
                for half in range(2):
                    if half == 0:
                        o = part[n, j, half, 1 - my, mx].astype(F32) + rs_one[n, j, half, 1 - my].astype(F32)
                    else:
                        o = part[n, j, half, my, 1 - mx].astype(F32) + rs_one[n, j, half, 1 - mx].astype(F32)
                    rs_mid[n, j, half] = o.astype(BF16)
                    stage_two(n, j, half).start()

    def collect(j):
        with scope("collect"):
            @pl.loop(0, no)
            def _(n):
                settle(rs_two.at[n, j], two_recv.at[j, n])
                for half in range(2):
                    o = part[n, j, half, my, mx].astype(F32) + rs_one[n, j, half, my if half == 0 else mx].astype(F32)
                    o = o + rs_two[n, j, half].astype(F32)
                    out_ref[:, j, pl.ds(pl.multiple_of(n * oc + half * hc, hc), hc)] = o.astype(BF16)

    @pl.when(low)
    def _():
        with scope("outp"):
            project((0, 1), True)

    @pl.when(high)
    def _():
        for j in range(2):
            with scope("merge"):
                @pl.when(z == 2)
                def _():
                    merge(j, 1)

                @pl.when(z == 3)
                def _():
                    merge(j, 2)

            with scope("outp"):
                project((j,), j == 0)

    for j in range(2):
        forward(j)
    for j in range(2):
        collect(j)

    _t = scope("tail")
    _t.__enter__()
    settle(rs_one, one_send)
    settle(rs_mid, two_send)
    for g in range(2):
        settle(sums_in.at[g], sum_send.at[g])

    lifted, others = pl.ds(0, LIFT), pl.ds(LIFT, nc - LIFT)
    own_rows = pl.ds(0, tok)

    @pl.when(z == 0)
    def _():
        for i, part_of in enumerate((pl.ds(0, nc), lifted)):
            settle(sums_far.at[0], far_send.at[i])
            settle(qk.at[0, part_of, :, own_rows], k_send.at[i])
            settle(vbuf.at[part_of, :, own_rows], v_send.at[i])

    @pl.when(z == 1)
    def _():
        settle(sums_far.at[0], far_send.at[0])
        settle(qk.at[0, lifted, :, own_rows], k_send.at[1])
        settle(vbuf.at[lifted, :, own_rows], v_send.at[1])
        for i in range(2):
            settle(lse_msg, l_send.at[i])
            settle(oout.at[i, others], o_send.at[i])

    @pl.when(z == 2)
    def _():
        settle(sums_far.at[0], far_send.at[0])
        settle(lse_msg, l_send.at[0])
        settle(oout.at[0], o_send.at[0])
        settle(qk.at[1, others, :, own_rows], q_send.at[0])

    @pl.when(z == 3)
    def _():
        for i in range(2):
            settle(sums_far.at[0], far_send.at[i])
        settle(qk.at[1, :, :, own_rows], q_send.at[0])
        settle(qk.at[1, others, :, own_rows], q_send.at[1])

    _t.__exit__(None, None, None)


def fused(ns, nt, tokens, w_query, w_key, w_value, w_out, gain_query, gain_key):
    tok, seqs, depth = tokens.shape
    local = w_query.shape[1]
    nc = local // COLS
    oc = 1024
    no = depth // oc
    rows = tok * seqs
    width = HEADS * HEAD_DIM
    vm = pltpu.VMEM
    dma = pltpu.SemaphoreType.DMA
    scratch = [
        vm((local,), F32), vm((local,), F32),
        vm((RING, depth, COLS), BF16), vm((no, local, oc), BF16),
        vm((tok, seqs, depth), BF16), vm((rows, depth), BF16), vm((rows, depth), BF16),
        vm((rows, HEAD_DIM), F32), vm((rows, HEAD_DIM), F32), vm((2, nc, 1, COLS), F32), vm((2, rows, HEAD_DIM), F32),
        vm((2, 8, rows), F32), vm((2, nt - 1, 8, rows), F32), vm((3, nt, 8, rows), F32),
        vm((3, rows, 2 * rows), F32), vm((2, 8, 2 * rows), F32),
        vm((2, nc, seqs, 3 * tok, COLS), BF16), vm((nc, seqs, 3 * tok, COLS), BF16),
        vm((nc, seqs, tok, COLS), F32), vm((seqs, tok, HEAD_DIM), F32),
        vm((2, nc, seqs, tok, COLS), BF16), vm((seqs, 2, tok, HEAD_DIM), F32), vm((seqs, 16, rows), F32),
        vm((2, nc, seqs, tok, COLS), BF16), vm((2, seqs, 16, rows), F32), vm((3, tok, HEAD_DIM), F32),
        vm((rows, local), BF16), vm((no, seqs, 2, 2, 2, tok // nt, oc // 2), BF16),
        vm((no, seqs, 2, 2, tok // nt, oc // 2), BF16), vm((no, seqs, 2, tok // nt, oc // 2), BF16), vm((no, seqs, 2, tok // nt, oc // 2), BF16),
        dma, dma((2,)), dma((RING,)), dma((no,)), dma((2,)), dma((2,)), dma((2,)), dma((3,)), dma((2,)), dma((2,)), dma((2, nc)),
        dma((2,)), dma((2, nc)), dma((2,)), dma((2, nc)), dma((2,)), dma((2,)), dma, dma((2, no)), dma, dma((2, no)),
    ]
    in_vmem = pl.BlockSpec(memory_space=pltpu.VMEM)
    in_hbm = pl.BlockSpec(memory_space=pltpu.HBM)
    return pl.pallas_call(
        functools.partial(block_kernel, ns, nt, tok, width),
        out_shape=pltpu.VMEM((tok // nt, seqs, depth), BF16),
        in_specs=[in_hbm] * 7,
        out_specs=in_vmem,
        scratch_shapes=scratch,
        compiler_params=pltpu.CompilerParams(collective_id=0, has_side_effects=True, vmem_limit_bytes=58 * 1024 * 1024),
    )(tokens, gain_query, gain_key, w_query, w_key, w_value, w_out)


def rotary(field, positions):
    half = HEAD_DIM // 2
    shaped = field.reshape(field.shape[0], -1, HEAD_DIM)
    freqs = jnp.exp(-jnp.log(500000.0) * jnp.arange(half, dtype=jnp.float32) * 2.0 / HEAD_DIM)
    angle = positions.astype(jnp.float32)[:, None] * freqs[None, :]
    cosine = jnp.cos(angle)[:, None, :]
    sine = jnp.sin(angle)[:, None, :]
    first = shaped[..., :half]
    second = shaped[..., half:]
    turned = jnp.concatenate(
        [first * cosine - second * sine, second * cosine + first * sine], axis=-1
    )
    return turned.reshape(field.shape[0], -1)


def local(tokens, w_query, w_key, w_value, w_out, gain_query, gain_key):
    tok_rows = tokens.shape[0]
    seq_count = tokens.shape[1]
    local_width = w_query.shape[1]
    local_heads = local_width // HEAD_DIM
    width = HEADS * HEAD_DIM
    flat = tokens.reshape(tok_rows * seq_count, tokens.shape[2])
    query = jnp.dot(flat, w_query, preferred_element_type=jnp.float32)
    key_raw = jnp.dot(flat, w_key, preferred_element_type=jnp.float32)
    sum_query, sum_key = lax.psum(
        (jnp.sum(query * query, axis=1), jnp.sum(key_raw * key_raw, axis=1)), "tensor"
    )
    value = jnp.dot(flat, w_value, preferred_element_type=jnp.float32).astype(jnp.bfloat16)
    scale_q = lax.rsqrt(sum_query / width + 1e-06)
    scale_k = lax.rsqrt(sum_key / width + 1e-06)
    my_block = lax.axis_index("seq")
    positions = my_block * tok_rows + jnp.arange(tok_rows, dtype=jnp.int32)
    row_positions = (positions[:, None] + jnp.zeros((1, seq_count), jnp.int32)).reshape(-1)
    q_normed = rotary(query * scale_q[:, None] * gain_query[None, :], row_positions).astype(
        jnp.bfloat16
    )
    k_normed = rotary(key_raw * scale_k[:, None] * gain_key[None, :], row_positions).astype(
        jnp.bfloat16
    )
    q_heads = q_normed.reshape(tok_rows, seq_count, local_heads, HEAD_DIM)
    k_local = k_normed.reshape(tok_rows, seq_count, local_width)
    v_local = value.reshape(tok_rows, seq_count, local_width)
    factor = HEAD_DIM ** (-0.5)
    piece = (
        lax.all_gather(k_local, "seq", axis=0, tiled=True),
        lax.all_gather(v_local, "seq", axis=0, tiled=True),
    )
    key_pos = jnp.arange(piece[0].shape[0], dtype=jnp.int32)
    key_block = piece[0]
    count = key_block.shape[0]
    key_heads = key_block.reshape(count, seq_count, local_heads, HEAD_DIM)
    value_heads = piece[1].reshape(count, seq_count, local_heads, HEAD_DIM)
    scores = (
        jnp.einsum("qshd,kshd->shqk", q_heads, key_heads, preferred_element_type=jnp.float32)
        * factor
    )
    allowed = (key_pos[None, None, None, :] <= positions[None, None, :, None]) & (
        key_pos[None, None, None, :] >= 0
    )
    old_max = jnp.full((seq_count, local_heads, tok_rows), -1e30, jnp.float32)
    new_max = jnp.maximum(old_max, jnp.max(jnp.where(allowed, scores, -1e30), axis=3))
    expo = jnp.where(allowed, jnp.exp(scores - new_max[..., None]), 0.0)
    new_total = jnp.sum(expo, axis=3)
    added = jnp.einsum(
        "shqk,kshd->shqd",
        expo.astype(jnp.bfloat16),
        value_heads,
        preferred_element_type=jnp.float32,
    )
    final_state = (new_max, new_total, added)
    final_max, final_total, final_acc = final_state
    mixed = (final_acc / final_total[..., None]).astype(jnp.bfloat16)
    mixed = jnp.transpose(mixed, (2, 0, 1, 3)).reshape(tok_rows, seq_count, local_width)
    return lax.psum_scatter(
        jnp.dot(mixed, w_out, preferred_element_type=jnp.float32).astype(jnp.bfloat16),
        "tensor",
        scatter_dimension=0,
        tiled=True,
    )


def solution(mesh):
    ns, nt = mesh.shape["seq"], mesh.shape["tensor"]
    step = functools.partial(fused, ns, nt) if ns == 4 and nt == 4 else local
    return jax.shard_map(
        step,
        mesh=mesh,
        in_specs=(
            P("seq", "dp", None),
            P(None, "tensor"),
            P(None, "tensor"),
            P(None, "tensor"),
            P("tensor", None),
            P("tensor"),
            P("tensor"),
        ),
        out_specs=P(("seq", "tensor"), "dp", None),
        check_vma=False,
    )
```

time: 45 us -> 40.7 us (0.904)
  Pallas kernels: 42.8 us -> 39.7 us
  local copies, waits for them, and re-layouts: 1.92 us -> 0.73 us
    pallas_call x1, Pallas kernels: 42.8 us -> 39.7 us  [fused(): pl.pallas_call(functools.partial(block_kernel, ns, nt, tok, width), out_s...]
    unnamed x1, local copies, waits for them, and re-layouts: 1.92 us -> 0.73 us
where the time goes in v2:
time: 40.7 us; the launch traced here: 40.5 us
  Pallas kernels  39.7 us (98%)
  local copies, waits for them, and re-layouts  0.73 us (2%)
    pallas_call x1, Pallas kernels, fused(): pl.pallas_call(functools.partial(block_kernel, ns, nt, tok, width), out_s...  39.7 us

profile of v2, /device:TPU:24, one launch (start us, length us, event | category | flops | bytes accessed | tf_op | source)
XLA Modules:
  0.0 40.5 jit_solution(18020366910892473174)
XLA Ops:
  0.0 39.7 %shard_map.73 = bf16[16,2,5120]{2,1,0:T(2,128)(2,1)S(1)} custom-call(bf16[64,2,5120]{2,1,0:T(2,128)(2,1)} %x_hbm.1, f32[1280]{0:T(1024)} %gq_hbm.1, f32[1280]{0:T(1024)} %gk_hbm.1, bf16[5120,1280]{1,0:T(8,128)(2,1)} %wq.1, bf16[5120,1280]{1,0:T(8,128)(2,1)} %wk.1, bf16[5120,1280]{1,0:T(8,128)(2,1)} %wv.1, bf16[1280,5120]{1,0:T(8,128)(2,1)} %wo.1), custom_call_target="tpu_custom_call" | custom-call | tf_op jit(solution)/shard_map/pallas_call | solution.py:755
  39.8 0.7 %copy.9 = bf16[16,2,5120]{2,1,0:T(2,128)(2,1)} copy(bf16[16,2,5120]{2,1,0:T(2,128)(2,1)S(1)} %shard_map.73) | data formatting | bytes 655360

commit v3 on v2

--- a/solution.py
+++ b/solution.py
@@ -13,7 +13,7 @@
 MESH = pl.DeviceIdType.MESH
 COLS = 2 * HEAD_DIM
 RING = 9
-LIFT = 1
+LIFT = (1, 1)
 F32 = jnp.float32
 BF16 = jnp.bfloat16
 
@@ -63,11 +63,11 @@
         def _():
             w_copy(wk, c, slot).start()
 
-        @pl.when(inside & ((low & (group == 1)) | (high & (group == 2))))
+        @pl.when(inside & (((z == 0) & (group == 1)) | ((z > 0) & (group == 2))))
         def _():
             w_copy(wv, c, slot).start()
 
-        @pl.when(inside & ((low & (group == 2)) | (high & (group == 0))))
+        @pl.when(inside & (((z == 0) & (group == 2)) | ((z == 1) & (group == 1)) | (high & (group == 0))))
         def _():
             w_copy(wq, c, slot).start()
 
@@ -104,6 +104,9 @@
     def settle(ref, sem):
         pltpu.make_async_copy(ref, ref, sem).wait()
 
+    def blocks(count):
+        return xi.at[:, pl.ds(0, count * HEAD_DIM)]
+
     def k_copy(c, j, b, to):
         at = b * tok
         return remote(qk.at[0, c, j, pl.ds(0, tok)], qk.at[0, c, j, pl.ds(at, tok)], k_send.at[to - 1], kv_recv.at[j, c], (dp, to, me))
@@ -124,8 +127,8 @@
     def near(g, d):
         return remote(sums_out.at[g], sums_in.at[g, d - 1], sum_send.at[g], sum_recv.at[g], (dp, z, lax.rem(me + d, nt)))
 
-    def far(d, slot, ss, to):
-        return remote(sums_out.at[0], sums_far.at[slot, d], far_send.at[ss], far_recv.at[slot], (dp, to, lax.rem(me + d, nt)))
+    def far(d, slot, ss, to, g=0):
+        return remote(sums_out.at[g], sums_far.at[slot, d], far_send.at[ss], far_recv.at[slot], (dp, to, lax.rem(me + d, nt)))
 
     def product(i):
         slot = lax.rem(i, RING)
@@ -207,6 +210,7 @@
         send_near(g)
 
     first = jnp.where(low, 0, 1)
+    second = jnp.where(z == 1, 1, 0)
 
     with scope("g0"):
         @pl.loop(0, nc)
@@ -219,19 +223,19 @@
 
             finish(acc, first, c)
 
-            @pl.when((z == 0) & (c < LIFT))
+            @pl.when((z == 0) & (c < LIFT[0]))
             def _():
                 k_copy(c, 0, 1, 2).start()
 
-            @pl.when((z == 0) & (c >= LIFT))
+            @pl.when((z == 0) & (c >= LIFT[0]))
             def _():
                 k_copy(c, 0, 1, 1).start()
 
-            @pl.when((z == 3) & (c < LIFT))
+            @pl.when((z == 3) & (c < LIFT[0]))
             def _():
                 q_copy(c, 0, 1, 2).start()
 
-            @pl.when((z == 3) & (c >= LIFT) & (c < nc - 2))
+            @pl.when((z == 3) & (c >= LIFT[0]) & (c < nc - 2))
             def _():
                 q_copy(c, 0, 2, 1).start()
 
@@ -274,9 +278,10 @@
 
     @pl.when(z == 1)
     def _():
-        @pl.loop(0, LIFT)
-        def _(c):
-            for j in range(2):
+        for j in range(2):
+
+            @pl.loop(0, LIFT[j])
+            def _(c):
                 k_copy(c, j, 2, 2).start()
 
     with scope("g1"):
@@ -284,42 +289,50 @@
         def _(c):
             acc = product(nc + c)
 
-            @pl.when(low)
+            @pl.when(z == 0)
             def _():
                 keep_value(acc, c)
 
-            @pl.when(high)
-            def _():
-                finish(acc, 0, c)
-
-            @pl.when((z == 0) & (c < LIFT))
+            @pl.when(z > 0)
+            def _():
+                finish(acc, second, c)
+
+            @pl.when((z == 0) & (c < LIFT[0]))
             def _():
                 v_copy(c, 0, 1, 2).start()
 
-            @pl.when((z == 0) & (c >= LIFT))
+            @pl.when((z == 0) & (c >= LIFT[0]))
             def _():
                 v_copy(c, 0, 1, 1).start()
 
-            @pl.when((z == 1) & (c < LIFT))
-            def _():
-                for j in range(2):
-                    v_copy(c, j, 2, 2).start()
-
-            @pl.when((z == 2) & (c >= LIFT))
+            @pl.when((z == 2) & (c >= LIFT[0]))
             def _():
                 q_copy(c, 0, 1, 1).start()
-
-            @pl.when((z == 3) & (c >= LIFT))
-            def _():
-                q_copy(c, 0, 1, 2).start()
-
-            @pl.when((z == 3) & (c < LIFT))
+                k_copy(c, 0, 1, 3).start()
+
+            @pl.when((z == 3) & (c < LIFT[1]))
             def _():
                 q_copy(c, 1, 1, 2).start()
 
-    @pl.when(high)
-    def _():
-        send_sums(1, 0)
+    @pl.when(z > 0)
+    def _():
+        fill_sums(1, second)
+
+        @pl.when(z == 2)
+        def _():
+            for d in range(nt):
+                far(d, 0, 1, 3, 1).start()
+
+        send_near(1)
+
+    @pl.when(z == 0)
+    def _():
+        for j, to in ((1, 2), (0, 1)):
+
+            @pl.loop(0, LIFT[j])
+            def _(c):
+                k_copy(c, j, 1, to).start()
+                v_copy(c, j, 1, to).start()
 
     def near_scale(g):
         settle(sums_in.at[g], sum_recv.at[g])
@@ -395,27 +408,21 @@
                 else:
                     own_lse[j] = jnp.where(lane == 2 * c, a, jnp.where(lane == 2 * c + 1, b, own_lse[j]))
 
+    def remote_wait(c, j):
+        with scope("attwait"):
+            settle(blocks(2), q_recv.at[j, c])
+            settle(blocks(2), kv_recv.at[j, c])
+
     def remote_part(c, j):
-        @pl.when(z == 1)
-        def _():
-            with scope("attwait"):
-                settle(qk.at[1, c, :, pl.ds(0, tok)], q_recv.at[j, c])
-                settle(qk.at[0, c, :, pl.ds(0, tok)], kv_recv.at[j, c])
-            attend(c, (j,), 1, 3, 2, False)
-            o_copy(c, j, 2, 3).start()
-            o_copy(c, j, 1, 2).start()
-
-        @pl.when(z == 2)
-        def _():
-            with scope("attwait"):
-                settle(qk.at[1, c, j, pl.ds(0, tok)], q_recv.at[j, c])
-            attend(c, (j,), 0, 2, 1, False)
-            o_copy(c, j, 1, 3).start()
+        remote_wait(c, j)
+        attend(c, (j,), 1, 3, 2, False)
+        o_copy(c, j, 2, 3).start()
+        o_copy(c, j, 1, 2).start()
 
     def lifted_part(c, j):
         with scope("liftwait"):
-            settle(qk.at[1, c, j, pl.ds(0, tok)], q_recv.at[j, c])
-            settle(qk.at[0, c, :, pl.ds(0, 2 * tok)], kv_recv.at[j, c])
+            settle(blocks(1), q_recv.at[j, c])
+            settle(blocks(4), kv_recv.at[j, c])
         attend(c, (j,), 0, 2, 3, True)
         o_copy(c, j, 1, 3).start()
 
@@ -439,29 +446,39 @@
         def _(c):
             acc = product(2 * nc + c)
 
-            @pl.when(low)
+            @pl.when(z == 0)
             def _():
                 finish(acc, 1, c)
 
-            @pl.when(high)
+            @pl.when(z > 0)
             def _():
                 keep_value(acc, c)
 
-            @pl.when((z == 0) & (c >= LIFT))
+            @pl.when((z == 0) & (c >= LIFT[1]))
             def _():
                 k_copy(c, 1, 1, 1).start()
                 v_copy(c, 1, 1, 1).start()
 
-            @pl.when((z == 2) & (c >= LIFT))
+            for j in range(2):
+
+                @pl.when((z == 1) & (c < LIFT[j]))
+                def _():
+                    v_copy(c, j, 2, 2).start()
+
+            @pl.when((z == 2) & (c >= LIFT[0]))
+            def _():
+                v_copy(c, 0, 1, 3).start()
+
+            @pl.when((z == 2) & (c >= LIFT[1]))
             def _():
                 q_copy(c, 1, 1, 1).start()
 
-            @pl.when((z == 3) & (c >= LIFT))
+            @pl.when((z == 3) & (c >= LIFT[1]))
             def _():
                 q_copy(c, 1, 2, 1).start()
                 q_copy(c, 1, 1, 2).start()
 
-            @pl.when((c == LIFT) & (z == 1))
+            @pl.when((c == LIFT[0]) & (z == 1))
             def _():
                 with scope("sw_near"):
                     a = near_scale(0)
@@ -469,73 +486,60 @@
                     set_rk(a, far_scale(0))
                 with scope("sw_far1"):
                     set_rq(1, far_scale(1))
+                remote_wait(c, 0)
+                attend(c, (0,), 1, 2, 2, False)
+                o_copy(c, 0, 1, 2).start()
                 with scope("sw_far2"):
                     set_rq(2, far_scale(2))
-
-            @pl.when((z == 1) & (c >= LIFT))
+                attend(c, (0,), 2, 3, 2, False)
+                o_copy(c, 0, 2, 3).start()
+
+            @pl.when((z == 1) & (c > LIFT[0]))
             def _():
                 remote_part(c, 0)
 
     @pl.when(z == 0)
     def _():
-        @pl.loop(0, LIFT)
+        @pl.loop(0, LIFT[1])
         def _(c):
-            k_copy(c, 1, 1, 2).start()
-            v_copy(c, 1, 1, 2).start()
-
-        @pl.loop(0, LIFT)
-        def _(c):
-            for j in range(2):
-                k_copy(c, j, 1, 1).start()
-                v_copy(c, j, 1, 1).start()
-
-    @pl.when(low)
-    def _():
+            k_copy(c, 1, 1, 1).start()
+            v_copy(c, 1, 1, 1).start()
+
         send_sums(1, 1)
 
-    @pl.when(high)
+    @pl.when(z == 1)
+    def _():
+        send_lse(0)
+
+    @pl.when(z == 2)
     def _():
         with scope("sw_near"):
             set_rq(0, near_scale(0))
             r = near_scale(1)
-
-        @pl.when(z == 3)
-        def _():
             set_rk(r, r)
-
-        @pl.when(z == 2)
-        def _():
-            with scope("sw_far"):
-                set_rk(r, far_scale(0), far_scale(1))
-                set_rq(1, far_scale(2))
-
-    with scope("rem0"):
-        @pl.when(z == 2)
-        def _():
-            @pl.loop(LIFT, nc)
+        with scope("own"):
+            @pl.loop(LIFT[0], nc)
             def _(c):
-                remote_part(c, 0)
-
-            @pl.loop(0, LIFT)
-            def _(c):
-                lifted_part(c, 0)
-
-        send_lse(0)
-
-    with scope("rem1"):
-        @pl.when((z == 1) | (z == 2))
-        def _():
-            @pl.loop(LIFT, nc)
-            def _(c):
-                remote_part(c, 1)
-
-        @pl.when(z == 2)
-        def _():
-            @pl.loop(0, LIFT)
-            def _(c):
-                lifted_part(c, 1)
-
-        send_lse(1)
+                attend(c, (0,), 0, 1, 1, False)
+
+        with scope("sw_far"):
+            set_rk(r, far_scale(0), far_scale(1))
+            set_rq(1, far_scale(2))
+        with scope("lift"):
+            for j in range(2):
+                if j == 1:
+
+                    @pl.loop(LIFT[1], nc)
+                    def _(c):
+                        settle(blocks(1), q_recv.at[1, c])
+                        attend(c, (1,), 0, 2, 1, False)
+                        o_copy(c, 1, 1, 3).start()
+
+                @pl.loop(0, LIFT[j])
+                def _(c):
+                    lifted_part(c, j)
+
+                send_lse(j)
 
     @pl.when(z == 0)
     def _():
@@ -547,30 +551,6 @@
             @pl.loop(0, nc)
             def _(c):
                 attend(c, (0, 1), 0, 1, 1, True)
-
-    @pl.when(z == 1)
-    def _():
-        with scope("own"):
-            set_rq(0, near_scale(1))
-
-            @pl.loop(0, nc)
-            def _(i):
-                c = lax.rem(i + LIFT, nc)
-
-                @pl.when(c < LIFT)
-                def _():
-                    with scope("ownwait"):
-                        for j in range(2):
-                            settle(qk.at[0, c, :, pl.ds(0, tok)], kv_recv.at[j, c])
-
-                attend(c, (0, 1), 0, 1, 2, True)
-
-    @pl.when(z == 3)
-    def _():
-        with scope("own"):
-            @pl.loop(0, nc)
-            def _(c):
-                attend(c, (0, 1), 0, 1, 1, False)
 
     def merge(j, ni):
         lses = [own_lse[j]]
@@ -584,24 +564,25 @@
         for s in range(ni + 1):
             shares[s] = parts[s] / tot
 
-        def blend(c, count):
-            settle(oin.at[pl.ds(0, count), c, j], o_recv.at[j, c])
+        def blend(c, slots):
+            settle(blocks(len(slots)), o_recv.at[j, c])
             for h in range(2):
                 hs = slice(h * HEAD_DIM, (h + 1) * HEAD_DIM)
                 o = 0.0
-                for s in range(count + 1):
+                for s in (0, *slots):
                     share = jnp.sum(jnp.where(lane == 2 * c + h, shares[s], 0.0), axis=1, keepdims=True)
                     o += share * (own_o[c, j, :, hs] if s == 0 else oin[s - 1, c, j, :, hs].astype(F32))
                 mixed[j * tok : (j + 1) * tok, pl.ds(pl.multiple_of(c * COLS + h * HEAD_DIM, HEAD_DIM), HEAD_DIM)] = o.astype(BF16)
 
         if ni == 2:
-            @pl.loop(0, LIFT)
+
+            @pl.loop(0, LIFT[j])
             def _(c):
-                blend(c, 1)
-
-        @pl.loop(LIFT, nc)
+                blend(c, (1,))
+
+        @pl.loop(LIFT[j], nc)
         def _(c):
-            blend(c, ni)
+            blend(c, (1,) if ni == 1 else (2,) if j == 0 else (1, 2))
 
     share = tok // nt
     hc = oc // 2
@@ -618,20 +599,22 @@
         to = 2 * (1 - my) + mx if half == 0 else 2 * my + 1 - mx
         return remote(rs_mid.at[n, j, half], rs_two.at[n, j, half], two_send, two_recv.at[j, n], (dp, z, to))
 
+    def project_part(n, js, first_pass):
+        lo, hi = js[0] * tok, (js[-1] + 1) * tok
+        if first_pass:
+            wo_copy(n).wait()
+        acc = jnp.dot(mixed[lo:hi], wov[n], preferred_element_type=F32).astype(BF16)
+        for j in js:
+            for half in range(2):
+                for t in range(nt):
+                    row = j * tok + t * share - lo
+                    part[n, j, half, t // 2, t % 2] = acc[row : row + share, half * hc : (half + 1) * hc]
+                stage_one(n, j, half).start()
+
     def project(js, first_pass):
-        lo, hi = js[0] * tok, (js[-1] + 1) * tok
-
         @pl.loop(0, no)
         def _(n):
-            if first_pass:
-                wo_copy(n).wait()
-            acc = jnp.dot(mixed[lo:hi], wov[n], preferred_element_type=F32).astype(BF16)
-            for j in js:
-                for half in range(2):
-                    for t in range(nt):
-                        row = j * tok + t * share - lo
-                        part[n, j, half, t // 2, t % 2] = acc[row : row + share, half * hc : (half + 1) * hc]
-                    stage_one(n, j, half).start()
+            project_part(n, js, first_pass)
 
     def forward(j):
         with scope("fwd"):
@@ -656,21 +639,79 @@
                     o = o + rs_two[n, j, half].astype(F32)
                     out_ref[:, j, pl.ds(pl.multiple_of(n * oc + half * hc, hc), hc)] = o.astype(BF16)
 
-    @pl.when(low)
+    @pl.when(z == 0)
     def _():
         with scope("outp"):
             project((0, 1), True)
 
+    @pl.when(z == 1)
+    def _():
+        def own(c, j):
+            @pl.when(c < LIFT[j])
+            def _():
+                with scope("ownwait"):
+                    settle(blocks(2), kv_recv.at[j, c])
+
+            attend(c, (j,), 0, 1, 2, True)
+
+        with scope("own0"):
+            set_rq(0, near_scale(1))
+
+            @pl.loop(0, nc)
+            def _(i):
+                own(lax.rem(i + LIFT[0], nc), 0)
+
+        with scope("rem1"):
+            @pl.loop(0, max(nc, no))
+            def _(i):
+                @pl.when((i >= LIFT[1]) & (i < nc))
+                def _():
+                    remote_part(i, 1)
+
+                @pl.when(i < no)
+                def _():
+                    project_part(i, (0,), True)
+
+            send_lse(1)
+
+        with scope("own1"):
+            @pl.loop(0, nc)
+            def _(i):
+                own(lax.rem(i + LIFT[1], nc), 1)
+
+        with scope("outp"):
+            project((1,), False)
+
     @pl.when(high)
     def _():
         for j in range(2):
-            with scope("merge"):
-                @pl.when(z == 2)
-                def _():
+            @pl.when(z == 2)
+            def _():
+                with scope("merge"):
                     merge(j, 1)
 
-                @pl.when(z == 3)
-                def _():
+            @pl.when(z == 3)
+            def _():
+                if j == 0:
+                    with scope("scales"):
+                        set_rq(0, near_scale(0))
+                        set_rk(near_scale(1), far_scale(0))
+                with scope("own"):
+                    alone = LIFT[0] if j == 0 else nc
+
+                    @pl.loop(0, alone)
+                    def _(c):
+                        attend(c, (j,), 0, 1, 1, False)
+
+                    if alone < nc:
+
+                        @pl.loop(alone, nc)
+                        def _(c):
+                            with scope("ownwait"):
+                                settle(blocks(2), kv_recv.at[j, c])
+                            attend(c, (j,), 0, 1, 2, False)
+
+                with scope("merge"):
                     merge(j, 2)
 
             with scope("outp"):
@@ -688,38 +729,40 @@
     for g in range(2):
         settle(sums_in.at[g], sum_send.at[g])
 
-    lifted, others = pl.ds(0, LIFT), pl.ds(LIFT, nc - LIFT)
-    own_rows = pl.ds(0, tok)
+    up = sum(LIFT)
+    down = 2 * nc - up
 
     @pl.when(z == 0)
     def _():
-        for i, part_of in enumerate((pl.ds(0, nc), lifted)):
+        for i, count in enumerate((2 * nc, up)):
             settle(sums_far.at[0], far_send.at[i])
-            settle(qk.at[0, part_of, :, own_rows], k_send.at[i])
-            settle(vbuf.at[part_of, :, own_rows], v_send.at[i])
+            settle(blocks(count), k_send.at[i])
+            settle(blocks(count), v_send.at[i])
 
     @pl.when(z == 1)
     def _():
         settle(sums_far.at[0], far_send.at[0])
-        settle(qk.at[0, lifted, :, own_rows], k_send.at[1])
-        settle(vbuf.at[lifted, :, own_rows], v_send.at[1])
+        settle(blocks(up), k_send.at[1])
+        settle(blocks(up), v_send.at[1])
         for i in range(2):
             settle(lse_msg, l_send.at[i])
-            settle(oout.at[i, others], o_send.at[i])
+            settle(blocks(down), o_send.at[i])
 
     @pl.when(z == 2)
-    def _():
-        settle(sums_far.at[0], far_send.at[0])
-        settle(lse_msg, l_send.at[0])
-        settle(oout.at[0], o_send.at[0])
-        settle(qk.at[1, others, :, own_rows], q_send.at[0])
-
-    @pl.when(z == 3)
     def _():
         for i in range(2):
             settle(sums_far.at[0], far_send.at[i])
-        settle(qk.at[1, :, :, own_rows], q_send.at[0])
-        settle(qk.at[1, others, :, own_rows], q_send.at[1])
+        settle(lse_msg, l_send.at[0])
+        settle(blocks(LIFT[0] + nc), o_send.at[0])
+        settle(blocks(down), q_send.at[0])
+        settle(blocks(nc - LIFT[0]), k_send.at[2])
+        settle(blocks(nc - LIFT[0]), v_send.at[2])
+
+    @pl.when(z == 3)
+    def _():
+        for i, count in enumerate((LIFT[0] + nc, down)):
+            settle(sums_far.at[0], far_send.at[i])
+            settle(blocks(count), q_send.at[i])
 
     _t.__exit__(None, None, None)
 
@@ -747,7 +790,7 @@
         vm((2, nc, seqs, tok, COLS), BF16), vm((2, seqs, 16, rows), F32), vm((3, tok, HEAD_DIM), F32),
         vm((rows, local), BF16), vm((no, seqs, 2, 2, 2, tok // nt, oc // 2), BF16),
         vm((no, seqs, 2, 2, tok // nt, oc // 2), BF16), vm((no, seqs, 2, tok // nt, oc // 2), BF16), vm((no, seqs, 2, tok // nt, oc // 2), BF16),
-        dma, dma((2,)), dma((RING,)), dma((no,)), dma((2,)), dma((2,)), dma((2,)), dma((3,)), dma((2,)), dma((2,)), dma((2, nc)),
+        dma, dma((2,)), dma((RING,)), dma((no,)), dma((2,)), dma((2,)), dma((2,)), dma((3,)), dma((3,)), dma((3,)), dma((2, nc)),
         dma((2,)), dma((2, nc)), dma((2,)), dma((2, nc)), dma((2,)), dma((2,)), dma, dma((2, no)), dma, dma((2, no)),
     ]
     in_vmem = pl.BlockSpec(memory_space=pltpu.VMEM)

time: 40.7 us -> 39.3 us (0.966)
  Pallas kernels: 39.7 us -> 38.3 us
    pallas_call x1, Pallas kernels: 39.7 us -> 38.3 us  [fused(): pl.pallas_call(functools.partial(block_kernel, ns, nt, tok, width), out_s...]
where the time goes in v3:
time: 39.3 us; the launch traced here: 39 us
  Pallas kernels  38.3 us (97%)
  local copies, waits for them, and re-layouts  0.73 us (2%)
    pallas_call x1, Pallas kernels, fused(): pl.pallas_call(functools.partial(block_kernel, ns, nt, tok, width), out_s...  38.3 us

profile of v3, /device:TPU:24, one launch (start us, length us, event | category | flops | bytes accessed | tf_op | source)
XLA Modules:
  0.0 39.0 jit_solution(11249255814160755129)
XLA Ops:
  0.0 38.3 %shard_map.73 = bf16[16,2,5120]{2,1,0:T(2,128)(2,1)S(1)} custom-call(bf16[64,2,5120]{2,1,0:T(2,128)(2,1)} %x_hbm.1, f32[1280]{0:T(1024)} %gq_hbm.1, f32[1280]{0:T(1024)} %gk_hbm.1, bf16[5120,1280]{1,0:T(8,128)(2,1)} %wq.1, bf16[5120,1280]{1,0:T(8,128)(2,1)} %wk.1, bf16[5120,1280]{1,0:T(8,128)(2,1)} %wv.1, bf16[1280,5120]{1,0:T(8,128)(2,1)} %wo.1), custom_call_target="tpu_custom_call" | custom-call | tf_op jit(solution)/shard_map/pallas_call | solution.py:798
  38.3 0.7 %copy.9 = bf16[16,2,5120]{2,1,0:T(2,128)(2,1)} copy(bf16[16,2,5120]{2,1,0:T(2,128)(2,1)S(1)} %shard_map.73) | data formatting | bytes 655360

commit v4 on v3

--- a/solution.py
+++ b/solution.py
@@ -612,7 +612,7 @@
                 stage_one(n, j, half).start()
 
     def project(js, first_pass):
-        @pl.loop(0, no)
+        @pl.loop(0, no, unroll=not first_pass)
         def _(n):
             project_part(n, js, first_pass)
 

time: 39.3 us -> 39.3 us (level)
  no operation moved by 1% of the time
where the time goes in v4:
time: 39.3 us; the launch traced here: 39 us
  Pallas kernels  38.3 us (97%)
  local copies, waits for them, and re-layouts  0.73 us (2%)
    pallas_call x1, Pallas kernels, fused(): pl.pallas_call(functools.partial(block_kernel, ns, nt, tok, width), out_s...  38.3 us

profile of v4, /device:TPU:24, one launch (start us, length us, event | category | flops | bytes accessed | tf_op | source)
XLA Modules:
  0.0 39.0 jit_solution(2653716481186983819)
XLA Ops:
  0.0 38.3 %shard_map.73 = bf16[16,2,5120]{2,1,0:T(2,128)(2,1)S(1)} custom-call(bf16[64,2,5120]{2,1,0:T(2,128)(2,1)} %x_hbm.1, f32[1280]{0:T(1024)} %gq_hbm.1, f32[1280]{0:T(1024)} %gk_hbm.1, bf16[5120,1280]{1,0:T(8,128)(2,1)} %wq.1, bf16[5120,1280]{1,0:T(8,128)(2,1)} %wk.1, bf16[5120,1280]{1,0:T(8,128)(2,1)} %wv.1, bf16[1280,5120]{1,0:T(8,128)(2,1)} %wo.1), custom_call_target="tpu_custom_call" | custom-call | tf_op jit(solution)/shard_map/pallas_call | solution.py:798
  38.3 0.7 %copy.9 = bf16[16,2,5120]{2,1,0:T(2,128)(2,1)} copy(bf16[16,2,5120]{2,1,0:T(2,128)(2,1)S(1)} %shard_map.73) | data formatting | bytes 655360
